TPU v7x, 128 devices: a whole 4x4x4 slice. The times are simulated.
128 devices in a mesh: pp: 2 (over core), dp: 64 (over z, y, x).
Axes of the slice: x: 4, y: 4, z: 4, core: 2. Of those that a mesh axis runs over, the one named last changes fastest.
Arguments:
- x_in: bfloat16 [12, 64, 128, 512], P(None, 'dp')
- seed_grad: bfloat16 [12, 64, 128, 512], P(None, 'dp')
- w_qkv: bfloat16 [4, 512, 1536], P('pp')
- w_out: bfloat16 [4, 512, 512], P('pp')
- w_up: bfloat16 [4, 512, 2048], P('pp')
- w_down: bfloat16 [4, 2048, 512], P('pp')
Outputs:
- output 1: bfloat16 [12, 64, 128, 512], P(None, 'dp')
- output 2: float32 [4, 512, 1536], P('pp', 'dp')
- output 3: float32 [4, 512, 512], P('pp', 'dp')
- output 4: float32 [4, 512, 2048], P('pp', 'dp')
- output 5: float32 [4, 2048, 512], P('pp', 'dp')
All inputs are finite; a program needn't handle non-finite values.
Results may differ from a plain program's by a relative error of at most 0.02.
Values are sent between devices in bfloat16 or wider.
A program may use at most 1 GiB of HBM per device.

v0:
```python
import jax
import jax.numpy as jnp
from jax import lax
from jax.sharding import PartitionSpec as P, NamedSharding

HEAD_DIM = 64
NORM_EPS = 1e-6
CONTRACT_COLS = (((1,), (1,)), ((), ()))
CONTRACT_ROWS = (((0,), (0,)), ((), ()))


def rms_forward(h_f32):
    return h_f32 * lax.rsqrt(jnp.mean(h_f32 * h_f32, axis=-1, keepdims=True) + NORM_EPS)


def rms_backward(h_f32, grad_f32):
    inv_rms = lax.rsqrt(jnp.mean(h_f32 * h_f32, axis=-1, keepdims=True) + NORM_EPS)
    normed = h_f32 * inv_rms
    return inv_rms * (grad_f32 - normed * jnp.mean(grad_f32 * normed, axis=-1, keepdims=True))


def gelu_tanh(up_f32):
    return jax.nn.gelu(up_f32, approximate=True)


def causal_probs(q_heads, k_heads):
    seq_len = q_heads.shape[1]
    scores = jnp.einsum("bqhe,bkhe->bhqk", q_heads, k_heads, preferred_element_type=jnp.float32) * HEAD_DIM ** -0.5
    allowed = lax.broadcasted_iota(jnp.int32, (seq_len, seq_len), 0) >= lax.broadcasted_iota(jnp.int32, (seq_len, seq_len), 1)
    return jax.nn.softmax(jnp.where(allowed, scores, -1e30), axis=-1)


def layer_forward(h_in, layer_w, batch_rows):
    w_qkv, w_out, w_up, w_down = layer_w
    tokens, model_width = h_in.shape
    head_shape = (batch_rows, tokens // batch_rows, model_width // HEAD_DIM, HEAD_DIM)
    h_f32 = h_in.astype(jnp.float32)
    a_norm = rms_forward(h_f32).astype(jnp.bfloat16)
    qkv_act = jnp.dot(a_norm, w_qkv, preferred_element_type=jnp.float32).astype(jnp.bfloat16)
    q_heads = qkv_act[:, :model_width].reshape(head_shape)
    k_heads = qkv_act[:, model_width:2 * model_width].reshape(head_shape)
    v_heads = qkv_act[:, 2 * model_width:].reshape(head_shape)
    attn_probs = causal_probs(q_heads, k_heads)
    attn_out = jnp.einsum("bhqk,bkhe->bqhe", attn_probs.astype(jnp.bfloat16), v_heads, preferred_element_type=jnp.float32).astype(jnp.bfloat16).reshape(tokens, model_width)
    h_mid = (h_f32 + jnp.dot(attn_out, w_out, preferred_element_type=jnp.float32)).astype(jnp.bfloat16)
    mid_f32 = h_mid.astype(jnp.float32)
    c_norm = rms_forward(mid_f32).astype(jnp.bfloat16)
    up_act = jnp.dot(c_norm, w_up, preferred_element_type=jnp.float32).astype(jnp.bfloat16)
    gelu_act = gelu_tanh(up_act.astype(jnp.float32)).astype(jnp.bfloat16)
    h_out = (mid_f32 + jnp.dot(gelu_act, w_down, preferred_element_type=jnp.float32)).astype(jnp.bfloat16)
    saved_acts = (a_norm, q_heads, k_heads, v_heads, attn_probs, attn_out, h_mid, c_norm, up_act, gelu_act)
    return h_out, saved_acts


def layer_input_grad(d_out, h_in, saved_acts, layer_w):
    w_qkv, w_out, w_up, w_down = layer_w
    a_norm, q_heads, k_heads, v_heads, attn_probs, attn_out, h_mid, c_norm, up_act, gelu_act = saved_acts
    tokens, model_width = d_out.shape
    d_gelu = lax.dot_general(d_out, w_down, CONTRACT_COLS, preferred_element_type=jnp.float32)
    gelu_vjp = jax.vjp(gelu_tanh, up_act.astype(jnp.float32))[1]
    d_up = gelu_vjp(d_gelu)[0].astype(jnp.bfloat16)
    d_cnorm = lax.dot_general(d_up, w_up, CONTRACT_COLS, preferred_element_type=jnp.float32)
    d_mid = (d_out.astype(jnp.float32) + rms_backward(h_mid.astype(jnp.float32), d_cnorm)).astype(jnp.bfloat16)
    d_attn = lax.dot_general(d_mid, w_out, CONTRACT_COLS, preferred_element_type=jnp.float32).astype(jnp.bfloat16).reshape(q_heads.shape)
    d_probs = jnp.einsum("bqhe,bkhe->bhqk", d_attn, v_heads, preferred_element_type=jnp.float32)
    d_vals = jnp.einsum("bhqk,bqhe->bkhe", attn_probs.astype(jnp.bfloat16), d_attn, preferred_element_type=jnp.float32).astype(jnp.bfloat16)
    d_scores = (attn_probs * (d_probs - jnp.sum(attn_probs * d_probs, axis=-1, keepdims=True)) * HEAD_DIM ** -0.5).astype(jnp.bfloat16)
    d_query = jnp.einsum("bhqk,bkhe->bqhe", d_scores, k_heads, preferred_element_type=jnp.float32).astype(jnp.bfloat16)
    d_key = jnp.einsum("bhqk,bqhe->bkhe", d_scores, q_heads, preferred_element_type=jnp.float32).astype(jnp.bfloat16)
    d_qkv = jnp.concatenate([d_query.reshape(tokens, model_width), d_key.reshape(tokens, model_width), d_vals.reshape(tokens, model_width)], axis=1)
    d_anorm = lax.dot_general(d_qkv, w_qkv, CONTRACT_COLS, preferred_element_type=jnp.float32)
    d_in = (d_mid.astype(jnp.float32) + rms_backward(h_in.astype(jnp.float32), d_anorm)).astype(jnp.bfloat16)
    return d_in, (a_norm, d_qkv, attn_out, d_mid, c_norm, d_up, gelu_act, d_out)


def layer_weight_grad(grad_parts):
    a_norm, d_qkv, attn_out, d_mid, c_norm, d_up, gelu_act, d_out = grad_parts
    return (
        lax.dot_general(a_norm, d_qkv, CONTRACT_ROWS, preferred_element_type=jnp.float32),
        lax.dot_general(attn_out, d_mid, CONTRACT_ROWS, preferred_element_type=jnp.float32),
        lax.dot_general(c_norm, d_up, CONTRACT_ROWS, preferred_element_type=jnp.float32),
        lax.dot_general(gelu_act, d_out, CONTRACT_ROWS, preferred_element_type=jnp.float32),
    )


def solution(mesh):
    num_stages = mesh.shape["pp"]
    slots = 2 * num_stages - 1
    fwd_pairs = [(sender, sender + 1) for sender in range(num_stages - 1)]
    bwd_pairs = [(sender + 1, sender) for sender in range(num_stages - 1)]

    def device_step(x_in, seed_grad, w_qkv, w_out, w_up, w_down):
        num_micro, batch_rows, seq_len, model_width = x_in.shape
        tokens = batch_rows * seq_len
        num_layers = w_qkv.shape[0]
        stage_idx = lax.axis_index("pp")
        is_first = stage_idx == 0
        is_last = stage_idx == num_stages - 1
        layer_ws = [(w_qkv[layer_idx], w_out[layer_idx], w_up[layer_idx], w_down[layer_idx]) for layer_idx in range(num_layers)]
        x_rows = x_in.reshape(num_micro, tokens, model_width)
        g_rows = seed_grad.reshape(num_micro, tokens, model_width)

        def tick(tick_idx, loop_state):
            recv_fwd, recv_bwd, saved_inputs, y_buf, grad_accs = loop_state
            f_micro = tick_idx - stage_idx
            b_micro = tick_idx - (2 * num_stages - 2) + stage_idx
            f_valid = (f_micro >= 0) & (f_micro < num_micro)
            b_valid = (b_micro >= 0) & (b_micro < num_micro)
            f_micro = jnp.clip(f_micro, 0, num_micro - 1)
            b_micro = jnp.clip(b_micro, 0, num_micro - 1)
            h_first = jnp.where(is_first, lax.dynamic_index_in_dim(x_rows, f_micro, 0, keepdims=False), recv_fwd)

            def run_forward(operands):
                h_cur, stash_in, y_in = operands
                layer_inputs = []
                for layer_w in layer_ws:
                    layer_inputs.append(h_cur)
                    h_cur = layer_forward(h_cur, layer_w, batch_rows)[0]
                stash_new = lax.dynamic_update_index_in_dim(stash_in, jnp.stack(layer_inputs), f_micro % slots, 0)
                y_new = lax.dynamic_update_index_in_dim(y_in, h_cur, f_micro, 0)
                return h_cur, stash_new, y_new

            send_fwd, saved_inputs, y_buf = lax.cond(f_valid, run_forward, lambda operands: operands, (h_first, saved_inputs, y_buf))
            d_last = jnp.where(is_last, lax.dynamic_index_in_dim(g_rows, b_micro, 0, keepdims=False), recv_bwd)

            def run_backward(operands):
                d_hid, accs_in = operands
                layer_inputs = lax.dynamic_index_in_dim(saved_inputs, b_micro % slots, 0, keepdims=False)
                accs_new = list(accs_in)
                for layer_idx in reversed(range(num_layers)):
                    h_in = layer_inputs[layer_idx]
                    saved_acts = layer_forward(h_in, layer_ws[layer_idx], batch_rows)[1]
                    d_hid, grad_parts = layer_input_grad(d_hid, h_in, saved_acts, layer_ws[layer_idx])
                    layer_grads = layer_weight_grad(grad_parts)
                    accs_new[layer_idx] = tuple(grad_acc + new_grad for grad_acc, new_grad in zip(accs_new[layer_idx], layer_grads))
                return d_hid, tuple(accs_new)

            send_bwd, grad_accs = lax.cond(b_valid, run_backward, lambda operands: operands, (d_last, grad_accs))
            recv_fwd = lax.ppermute(send_fwd, "pp", fwd_pairs)
            recv_bwd = lax.ppermute(send_bwd, "pp", bwd_pairs)
            return recv_fwd, recv_bwd, saved_inputs, y_buf, grad_accs

        act_zero = jnp.zeros((tokens, model_width), jnp.bfloat16)
        init_state = (
            act_zero,
            act_zero,
            jnp.zeros((slots, num_layers, tokens, model_width), jnp.bfloat16),
            jnp.zeros((num_micro, tokens, model_width), jnp.bfloat16),
            tuple(tuple(jnp.zeros(weight.shape, jnp.float32) for weight in layer_w) for layer_w in layer_ws),
        )
        final_state = lax.fori_loop(0, num_micro + 2 * num_stages - 2, tick, init_state)
        y_buf = final_state[3]
        grad_accs = final_state[4]
        y_full = lax.psum(jnp.where(is_last, y_buf, jnp.zeros_like(y_buf)), "pp")
        grad_shards = [
            lax.psum_scatter(jnp.stack([grad_accs[layer_idx][weight_idx] for layer_idx in range(num_layers)]), "dp", scatter_dimension=1, tiled=True)
            for weight_idx in range(4)
        ]
        return (y_full.reshape(x_in.shape), grad_shards[0], grad_shards[1], grad_shards[2], grad_shards[3])

    act_spec = P(None, "dp")
    weight_spec = P("pp")
    grad_spec = P("pp", "dp")
    return jax.shard_map(
        device_step,
        mesh=mesh,
        in_specs=(act_spec, act_spec, weight_spec, weight_spec, weight_spec, weight_spec),
        out_specs=(act_spec, grad_spec, grad_spec, grad_spec, grad_spec),
        check_vma=False,
    )
```

profile of v0, /device:TPU:1, one launch (start us, length us, event | category | flops | bytes accessed | tf_op | source)
XLA Modules:
  0.0 3156.2 jit_solution(5424486972316802029)
XLA Ops:
  38.7 1826.5 %while.37 = (s32[]{:T(128)}, bf16[128,512]{1,0:T(8,128)(2,1)}, bf16[128,512]{1,0:T(8,128)(2,1)S(1)}, bf16[3,2,128,512]{3,2,1,0:T(8,128)(2,1)}, bf16[12,128,512]{...) while((s32[]{:T(128)}, bf16[128,512]{1,0:T(8,128)(2,1)}, ...), condition=%wide.region_27.28_spmd, body=%wide.region_0.27_spmd.sunk | while | flops 6327153152 | bytes 395652032 | solution.py:151
  42.4 40.4 %collective-permute-start.1 = (bf16[128,512]{1,0:T(8,128)(2,1)}, bf16[128,512]{1,0:T(8,128)(2,1)S(1)}, u32[]{:S(2)}, u32[]{:S(2)}) collective-permute-start(bf16[128,512]{1,0:T(8,128)(2,1)} %get-tuple-element.1075), channel_id=1, source_target_pairs={{64,0},{65,1},{66,2},{67,3},{68,4},{69,5},{70,6},{71,7},{72,8},{73... | collective-permute-start | bytes 393224 | tf_op jit(solution)/shard_map/while/body/eval_jaxpr/ppermute | solution.py:140
  84.8 37.3 %conditional.4 = (bf16[128,512]{1,0:T(8,128)(2,1)}, bf16[3,2,128,512]{3,2,1,0:T(8,128)(2,1)}, bf16[12,128,512]{2,1,0:T(8,128)(2,1)}) conditional(s32[]{:T(128)} %convert_element_type.476, (bf16[128,512]{1,0:T(8,128)(2,1)S(1)}, bf16[3,2,128,512]{3,2,1,0:T(8,128)(2,1)}, bf16[12,128,512]{2,1,0:T(8,128)(2,1)}) %tuple.89, ...), branch_computations={%region_1.1_spmd, %region_2.10_spmd} | conditional | flops 1722567680 | bytes 23437468 | solution.py:123
  117.4 4.0 bitcast_dynamic-update-slice_fusion
  123.4 95.8 %conditional.5 = (bf16[128,512]{1,0:T(8,128)(2,1)}, f32[512,1536]{1,0:T(8,128)}, f32[512,512]{1,0:T(8,128)}, f32[512,2048]{1,0:T(8,128)}, f32[2048,512]{1,0:T(8,...) conditional(s32[]{:T(128)} %convert_element_type.477, ...), branch_computations={%region_11.11_spmd, %region_12.26_spmd} | conditional | flops 4604454400 | bytes 370378720 | solution.py:138
  138.7 4.0 fusion.97
  222.5 37.3 %conditional.4 = (bf16[128,512]{1,0:T(8,128)(2,1)}, bf16[3,2,128,512]{3,2,1,0:T(8,128)(2,1)}, bf16[12,128,512]{2,1,0:T(8,128)(2,1)}) conditional(s32[]{:T(128)} %convert_element_type.476, (bf16[128,512]{1,0:T(8,128)(2,1)S(1)}, bf16[3,2,128,512]{3,2,1,0:T(8,128)(2,1)}, bf16[12,128,512]{2,1,0:T(8,128)(2,1)}) %tuple.89, ...), branch_computations={%region_1.1_spmd, %region_2.10_spmd} | conditional | flops 1722567680 | bytes 23437468 | solution.py:123
  255.1 4.0 bitcast_dynamic-update-slice_fusion
  261.1 95.8 %conditional.5 = (bf16[128,512]{1,0:T(8,128)(2,1)}, f32[512,1536]{1,0:T(8,128)}, f32[512,512]{1,0:T(8,128)}, f32[512,2048]{1,0:T(8,128)}, f32[2048,512]{1,0:T(8,...) conditional(s32[]{:T(128)} %convert_element_type.477, ...), branch_computations={%region_11.11_spmd, %region_12.26_spmd} | conditional | flops 4604454400 | bytes 370378720 | solution.py:138
  276.4 4.0 fusion.97
  362.5 37.3 %conditional.4 = (bf16[128,512]{1,0:T(8,128)(2,1)}, bf16[3,2,128,512]{3,2,1,0:T(8,128)(2,1)}, bf16[12,128,512]{2,1,0:T(8,128)(2,1)}) conditional(s32[]{:T(128)} %convert_element_type.476, (bf16[128,512]{1,0:T(8,128)(2,1)S(1)}, bf16[3,2,128,512]{3,2,1,0:T(8,128)(2,1)}, bf16[12,128,512]{2,1,0:T(8,128)(2,1)}) %tuple.89, ...), branch_computations={%region_1.1_spmd, %region_2.10_spmd} | conditional | flops 1722567680 | bytes 23437468 | solution.py:123
  395.1 4.0 bitcast_dynamic-update-slice_fusion
  401.1 95.8 %conditional.5 = (bf16[128,512]{1,0:T(8,128)(2,1)}, f32[512,1536]{1,0:T(8,128)}, f32[512,512]{1,0:T(8,128)}, f32[512,2048]{1,0:T(8,128)}, f32[2048,512]{1,0:T(8,...) conditional(s32[]{:T(128)} %convert_element_type.477, ...), branch_computations={%region_11.11_spmd, %region_12.26_spmd} | conditional | flops 4604454400 | bytes 370378720 | solution.py:138
  502.5 37.3 %conditional.4 = (bf16[128,512]{1,0:T(8,128)(2,1)}, bf16[3,2,128,512]{3,2,1,0:T(8,128)(2,1)}, bf16[12,128,512]{2,1,0:T(8,128)(2,1)}) conditional(s32[]{:T(128)} %convert_element_type.476, (bf16[128,512]{1,0:T(8,128)(2,1)S(1)}, bf16[3,2,128,512]{3,2,1,0:T(8,128)(2,1)}, bf16[12,128,512]{2,1,0:T(8,128)(2,1)}) %tuple.89, ...), branch_computations={%region_1.1_spmd, %region_2.10_spmd} | conditional | flops 1722567680 | bytes 23437468 | solution.py:123
  535.1 4.0 bitcast_dynamic-update-slice_fusion
  541.1 95.8 %conditional.5 = (bf16[128,512]{1,0:T(8,128)(2,1)}, f32[512,1536]{1,0:T(8,128)}, f32[512,512]{1,0:T(8,128)}, f32[512,2048]{1,0:T(8,128)}, f32[2048,512]{1,0:T(8,...) conditional(s32[]{:T(128)} %convert_element_type.477, ...), branch_computations={%region_11.11_spmd, %region_12.26_spmd} | conditional | flops 4604454400 | bytes 370378720 | solution.py:138
  642.6 37.3 %conditional.4 = (bf16[128,512]{1,0:T(8,128)(2,1)}, bf16[3,2,128,512]{3,2,1,0:T(8,128)(2,1)}, bf16[12,128,512]{2,1,0:T(8,128)(2,1)}) conditional(s32[]{:T(128)} %convert_element_type.476, (bf16[128,512]{1,0:T(8,128)(2,1)S(1)}, bf16[3,2,128,512]{3,2,1,0:T(8,128)(2,1)}, bf16[12,128,512]{2,1,0:T(8,128)(2,1)}) %tuple.89, ...), branch_computations={%region_1.1_spmd, %region_2.10_spmd} | conditional | flops 1722567680 | bytes 23437468 | solution.py:123
  675.1 4.0 bitcast_dynamic-update-slice_fusion
  681.1 95.8 %conditional.5 = (bf16[128,512]{1,0:T(8,128)(2,1)}, f32[512,1536]{1,0:T(8,128)}, f32[512,512]{1,0:T(8,128)}, f32[512,2048]{1,0:T(8,128)}, f32[2048,512]{1,0:T(8,...) conditional(s32[]{:T(128)} %convert_element_type.477, ...), branch_computations={%region_11.11_spmd, %region_12.26_spmd} | conditional | flops 4604454400 | bytes 370378720 | solution.py:138
  782.6 37.3 %conditional.4 = (bf16[128,512]{1,0:T(8,128)(2,1)}, bf16[3,2,128,512]{3,2,1,0:T(8,128)(2,1)}, bf16[12,128,512]{2,1,0:T(8,128)(2,1)}) conditional(s32[]{:T(128)} %convert_element_type.476, (bf16[128,512]{1,0:T(8,128)(2,1)S(1)}, bf16[3,2,128,512]{3,2,1,0:T(8,128)(2,1)}, bf16[12,128,512]{2,1,0:T(8,128)(2,1)}) %tuple.89, ...), branch_computations={%region_1.1_spmd, %region_2.10_spmd} | conditional | flops 1722567680 | bytes 23437468 | solution.py:123
  815.2 4.0 bitcast_dynamic-update-slice_fusion
  821.2 95.8 %conditional.5 = (bf16[128,512]{1,0:T(8,128)(2,1)}, f32[512,1536]{1,0:T(8,128)}, f32[512,512]{1,0:T(8,128)}, f32[512,2048]{1,0:T(8,128)}, f32[2048,512]{1,0:T(8,...) conditional(s32[]{:T(128)} %convert_element_type.477, ...), branch_computations={%region_11.11_spmd, %region_12.26_spmd} | conditional | flops 4604454400 | bytes 370378720 | solution.py:138
  922.6 37.3 %conditional.4 = (bf16[128,512]{1,0:T(8,128)(2,1)}, bf16[3,2,128,512]{3,2,1,0:T(8,128)(2,1)}, bf16[12,128,512]{2,1,0:T(8,128)(2,1)}) conditional(s32[]{:T(128)} %convert_element_type.476, (bf16[128,512]{1,0:T(8,128)(2,1)S(1)}, bf16[3,2,128,512]{3,2,1,0:T(8,128)(2,1)}, bf16[12,128,512]{2,1,0:T(8,128)(2,1)}) %tuple.89, ...), branch_computations={%region_1.1_spmd, %region_2.10_spmd} | conditional | flops 1722567680 | bytes 23437468 | solution.py:123
  955.2 4.0 bitcast_dynamic-update-slice_fusion
  961.2 95.8 %conditional.5 = (bf16[128,512]{1,0:T(8,128)(2,1)}, f32[512,1536]{1,0:T(8,128)}, f32[512,512]{1,0:T(8,128)}, f32[512,2048]{1,0:T(8,128)}, f32[2048,512]{1,0:T(8,...) conditional(s32[]{:T(128)} %convert_element_type.477, ...), branch_computations={%region_11.11_spmd, %region_12.26_spmd} | conditional | flops 4604454400 | bytes 370378720 | solution.py:138
  1062.6 37.3 %conditional.4 = (bf16[128,512]{1,0:T(8,128)(2,1)}, bf16[3,2,128,512]{3,2,1,0:T(8,128)(2,1)}, bf16[12,128,512]{2,1,0:T(8,128)(2,1)}) conditional(s32[]{:T(128)} %convert_element_type.476, (bf16[128,512]{1,0:T(8,128)(2,1)S(1)}, bf16[3,2,128,512]{3,2,1,0:T(8,128)(2,1)}, bf16[12,128,512]{2,1,0:T(8,128)(2,1)}) %tuple.89, ...), branch_computations={%region_1.1_spmd, %region_2.10_spmd} | conditional | flops 1722567680 | bytes 23437468 | solution.py:123
  1095.2 4.0 bitcast_dynamic-update-slice_fusion
  1101.2 95.8 %conditional.5 = (bf16[128,512]{1,0:T(8,128)(2,1)}, f32[512,1536]{1,0:T(8,128)}, f32[512,512]{1,0:T(8,128)}, f32[512,2048]{1,0:T(8,128)}, f32[2048,512]{1,0:T(8,...) conditional(s32[]{:T(128)} %convert_element_type.477, ...), branch_computations={%region_11.11_spmd, %region_12.26_spmd} | conditional | flops 4604454400 | bytes 370378720 | solution.py:138
  1202.7 37.3 %conditional.4 = (bf16[128,512]{1,0:T(8,128)(2,1)}, bf16[3,2,128,512]{3,2,1,0:T(8,128)(2,1)}, bf16[12,128,512]{2,1,0:T(8,128)(2,1)}) conditional(s32[]{:T(128)} %convert_element_type.476, (bf16[128,512]{1,0:T(8,128)(2,1)S(1)}, bf16[3,2,128,512]{3,2,1,0:T(8,128)(2,1)}, bf16[12,128,512]{2,1,0:T(8,128)(2,1)}) %tuple.89, ...), branch_computations={%region_1.1_spmd, %region_2.10_spmd} | conditional | flops 1722567680 | bytes 23437468 | solution.py:123
  1235.3 4.0 bitcast_dynamic-update-slice_fusion
  1241.3 95.8 %conditional.5 = (bf16[128,512]{1,0:T(8,128)(2,1)}, f32[512,1536]{1,0:T(8,128)}, f32[512,512]{1,0:T(8,128)}, f32[512,2048]{1,0:T(8,128)}, f32[2048,512]{1,0:T(8,...) conditional(s32[]{:T(128)} %convert_element_type.477, ...), branch_computations={%region_11.11_spmd, %region_12.26_spmd} | conditional | flops 4604454400 | bytes 370378720 | solution.py:138
  1342.7 37.3 %conditional.4 = (bf16[128,512]{1,0:T(8,128)(2,1)}, bf16[3,2,128,512]{3,2,1,0:T(8,128)(2,1)}, bf16[12,128,512]{2,1,0:T(8,128)(2,1)}) conditional(s32[]{:T(128)} %convert_element_type.476, (bf16[128,512]{1,0:T(8,128)(2,1)S(1)}, bf16[3,2,128,512]{3,2,1,0:T(8,128)(2,1)}, bf16[12,128,512]{2,1,0:T(8,128)(2,1)}) %tuple.89, ...), branch_computations={%region_1.1_spmd, %region_2.10_spmd} | conditional | flops 1722567680 | bytes 23437468 | solution.py:123
  1375.3 4.0 bitcast_dynamic-update-slice_fusion
  1381.3 95.8 %conditional.5 = (bf16[128,512]{1,0:T(8,128)(2,1)}, f32[512,1536]{1,0:T(8,128)}, f32[512,512]{1,0:T(8,128)}, f32[512,2048]{1,0:T(8,128)}, f32[2048,512]{1,0:T(8,...) conditional(s32[]{:T(128)} %convert_element_type.477, ...), branch_computations={%region_11.11_spmd, %region_12.26_spmd} | conditional | flops 4604454400 | bytes 370378720 | solution.py:138
  1482.7 37.3 %conditional.4 = (bf16[128,512]{1,0:T(8,128)(2,1)}, bf16[3,2,128,512]{3,2,1,0:T(8,128)(2,1)}, bf16[12,128,512]{2,1,0:T(8,128)(2,1)}) conditional(s32[]{:T(128)} %convert_element_type.476, (bf16[128,512]{1,0:T(8,128)(2,1)S(1)}, bf16[3,2,128,512]{3,2,1,0:T(8,128)(2,1)}, bf16[12,128,512]{2,1,0:T(8,128)(2,1)}) %tuple.89, ...), branch_computations={%region_1.1_spmd, %region_2.10_spmd} | conditional | flops 1722567680 | bytes 23437468 | solution.py:123
  1515.3 4.0 bitcast_dynamic-update-slice_fusion
  1521.3 95.8 %conditional.5 = (bf16[128,512]{1,0:T(8,128)(2,1)}, f32[512,1536]{1,0:T(8,128)}, f32[512,512]{1,0:T(8,128)}, f32[512,2048]{1,0:T(8,128)}, f32[2048,512]{1,0:T(8,...) conditional(s32[]{:T(128)} %convert_element_type.477, ...), branch_computations={%region_11.11_spmd, %region_12.26_spmd} | conditional | flops 4604454400 | bytes 370378720 | solution.py:138
  1622.8 37.3 %conditional.4 = (bf16[128,512]{1,0:T(8,128)(2,1)}, bf16[3,2,128,512]{3,2,1,0:T(8,128)(2,1)}, bf16[12,128,512]{2,1,0:T(8,128)(2,1)}) conditional(s32[]{:T(128)} %convert_element_type.476, (bf16[128,512]{1,0:T(8,128)(2,1)S(1)}, bf16[3,2,128,512]{3,2,1,0:T(8,128)(2,1)}, bf16[12,128,512]{2,1,0:T(8,128)(2,1)}) %tuple.89, ...), branch_computations={%region_1.1_spmd, %region_2.10_spmd} | conditional | flops 1722567680 | bytes 23437468 | solution.py:123
  1655.3 4.0 bitcast_dynamic-update-slice_fusion
  1661.3 95.8 %conditional.5 = (bf16[128,512]{1,0:T(8,128)(2,1)}, f32[512,1536]{1,0:T(8,128)}, f32[512,512]{1,0:T(8,128)}, f32[512,2048]{1,0:T(8,128)}, f32[2048,512]{1,0:T(8,...) conditional(s32[]{:T(128)} %convert_element_type.477, ...), branch_computations={%region_11.11_spmd, %region_12.26_spmd} | conditional | flops 4604454400 | bytes 370378720 | solution.py:138
  1765.4 98.8 %collective-permute-start.1 = (bf16[128,512]{1,0:T(8,128)(2,1)}, bf16[128,512]{1,0:T(8,128)(2,1)S(1)}, u32[]{:S(2)}, u32[]{:S(2)}) collective-permute-start(bf16[128,512]{1,0:T(8,128)(2,1)} %get-tuple-element.1075), channel_id=1, source_target_pairs={{64,0},{65,1},{66,2},{67,3},{68,4},{69,5},{70,6},{71,7},{72,8},{73... | collective-permute-start | bytes 393224 | tf_op jit(solution)/shard_map/while/body/eval_jaxpr/ppermute | solution.py:140
  1871.2 5.0 pad_maximum_fusion.8
  1876.2 7.8 pad_maximum_fusion.6
  1884.1 7.7 pad_maximum_fusion.7
  1895.7 284.2 %reduce-scatter.7.cloned.1.call-done = f32[2,8,512]{2,1,0:T(8,128)} async-done(((f32[2,512,512]{2,1,0:T(8,128)}), f32[2,8,512]{2,1,0:T(8,128)}) %reduce-scatter.7.cloned.1.call-update) | async-done | bytes 32784 | tf_op jit(solution)/shard_map/reduce_scatter | solution.py:156
  2179.9 274.9 %reduce-scatter.5.cloned.1.call-done = f32[2,8,1536]{2,1,0:T(8,128)} async-done(((f32[2,512,1536]{2,1,0:T(8,128)}), f32[2,8,1536]{2,1,0:T(8,128)}) %reduce-scatter.5.cloned.1.call-update) | async-done | bytes 98320 | tf_op jit(solution)/shard_map/reduce_scatter | solution.py:156
  2454.8 324.6 %reduce-scatter.9.cloned.1.call-done = f32[2,8,2048]{2,1,0:T(8,128)} async-done(((f32[2,512,2048]{2,1,0:T(8,128)}), f32[2,8,2048]{2,1,0:T(8,128)}) %reduce-scatter.9.cloned.1.call-update) | async-done | bytes 131088 | tf_op jit(solution)/shard_map/reduce_scatter | solution.py:156
  2779.4 366.6 %reduce-scatter.11.cloned.1.call-done = f32[2,32,512]{2,1,0:T(8,128)} async-done(((f32[2,2048,512]{2,1,0:T(8,128)}), f32[2,32,512]{2,1,0:T(8,128)}) %reduce-scatter.11.cloned.1.call-update) | async-done | bytes 131088 | tf_op jit(solution)/shard_map/reduce_scatter | solution.py:156
  (2498 shorter events, 1669.1 us)
Async XLA Ops:
  8.0 1887.7 %all-reduce.2.cloned.1.call-start = ((), (), s32[]{:S(2)}) async-start(), calls=%async_computation.4 | async-start | bytes 3145728 | tf_op jit(solution)/shard_map/psum | solution.py:154
  40.4 42.4 %collective-permute-start = (bf16[128,512]{1,0:T(8,128)(2,1)}, bf16[128,512]{1,0:T(8,128)(2,1)}, u32[]{:S(2)}, u32[]{:S(2)}) collective-permute-start(bf16[128,512]{1,0:T(8,128)(2,1)} %get-tuple-element.1072), channel_id=1, source_target_pairs={{0,64},{1,65},{2,66},{3,67},{4,68},{5,69},{6,70},{7,71},{8,72},{9,... | collective-permute-start | bytes 393224 | tf_op jit(solution)/shard_map/while/body/eval_jaxpr/ppermute | solution.py:139
  42.4 41.4 %collective-permute-start.1 = (bf16[128,512]{1,0:T(8,128)(2,1)}, bf16[128,512]{1,0:T(8,128)(2,1)S(1)}, u32[]{:S(2)}, u32[]{:S(2)}) collective-permute-start(bf16[128,512]{1,0:T(8,128)(2,1)} %get-tuple-element.1075), channel_id=1, source_target_pairs={{64,0},{65,1},{66,2},{67,3},{68,4},{69,5},{70,6},{71,7},{72,8},{73... | collective-permute-start | bytes 393224 | tf_op jit(solution)/shard_map/while/body/eval_jaxpr/ppermute | solution.py:140
  122.1 98.4 %collective-permute-start = (bf16[128,512]{1,0:T(8,128)(2,1)}, bf16[128,512]{1,0:T(8,128)(2,1)}, u32[]{:S(2)}, u32[]{:S(2)}) collective-permute-start(bf16[128,512]{1,0:T(8,128)(2,1)} %get-tuple-element.1072), channel_id=1, source_target_pairs={{0,64},{1,65},{2,66},{3,67},{4,68},{5,69},{6,70},{7,71},{8,72},{9,... | collective-permute-start | bytes 393224 | tf_op jit(solution)/shard_map/while/body/eval_jaxpr/ppermute | solution.py:139
  174.9 4.9 copy-start.15
  187.6 5.1 copy-start.51
  219.2 2.3 collective-permute-start.1
  259.8 100.7 %collective-permute-start = (bf16[128,512]{1,0:T(8,128)(2,1)}, bf16[128,512]{1,0:T(8,128)(2,1)}, u32[]{:S(2)}, u32[]{:S(2)}) collective-permute-start(bf16[128,512]{1,0:T(8,128)(2,1)} %get-tuple-element.1072), channel_id=1, source_target_pairs={{0,64},{1,65},{2,66},{3,67},{4,68},{5,69},{6,70},{7,71},{8,72},{9,... | collective-permute-start | bytes 393224 | tf_op jit(solution)/shard_map/while/body/eval_jaxpr/ppermute | solution.py:139
  325.3 5.1 copy-start.51
  356.8 4.6 collective-permute-start.1
  399.8 100.7 %collective-permute-start = (bf16[128,512]{1,0:T(8,128)(2,1)}, bf16[128,512]{1,0:T(8,128)(2,1)}, u32[]{:S(2)}, u32[]{:S(2)}) collective-permute-start(bf16[128,512]{1,0:T(8,128)(2,1)} %get-tuple-element.1072), channel_id=1, source_target_pairs={{0,64},{1,65},{2,66},{3,67},{4,68},{5,69},{6,70},{7,71},{8,72},{9,... | collective-permute-start | bytes 393224 | tf_op jit(solution)/shard_map/while/body/eval_jaxpr/ppermute | solution.py:139
  465.3 5.1 copy-start.51
  496.9 4.6 collective-permute-start.1
  539.8 100.7 %collective-permute-start = (bf16[128,512]{1,0:T(8,128)(2,1)}, bf16[128,512]{1,0:T(8,128)(2,1)}, u32[]{:S(2)}, u32[]{:S(2)}) collective-permute-start(bf16[128,512]{1,0:T(8,128)(2,1)} %get-tuple-element.1072), channel_id=1, source_target_pairs={{0,64},{1,65},{2,66},{3,67},{4,68},{5,69},{6,70},{7,71},{8,72},{9,... | collective-permute-start | bytes 393224 | tf_op jit(solution)/shard_map/while/body/eval_jaxpr/ppermute | solution.py:139
  605.4 5.1 copy-start.51
  636.9 4.6 collective-permute-start.1
  679.9 100.7 %collective-permute-start = (bf16[128,512]{1,0:T(8,128)(2,1)}, bf16[128,512]{1,0:T(8,128)(2,1)}, u32[]{:S(2)}, u32[]{:S(2)}) collective-permute-start(bf16[128,512]{1,0:T(8,128)(2,1)} %get-tuple-element.1072), channel_id=1, source_target_pairs={{0,64},{1,65},{2,66},{3,67},{4,68},{5,69},{6,70},{7,71},{8,72},{9,... | collective-permute-start | bytes 393224 | tf_op jit(solution)/shard_map/while/body/eval_jaxpr/ppermute | solution.py:139
  732.6 4.9 copy-start.15
  745.4 5.1 copy-start.51
  776.9 4.6 collective-permute-start.1
  819.9 100.7 %collective-permute-start = (bf16[128,512]{1,0:T(8,128)(2,1)}, bf16[128,512]{1,0:T(8,128)(2,1)}, u32[]{:S(2)}, u32[]{:S(2)}) collective-permute-start(bf16[128,512]{1,0:T(8,128)(2,1)} %get-tuple-element.1072), channel_id=1, source_target_pairs={{0,64},{1,65},{2,66},{3,67},{4,68},{5,69},{6,70},{7,71},{8,72},{9,... | collective-permute-start | bytes 393224 | tf_op jit(solution)/shard_map/while/body/eval_jaxpr/ppermute | solution.py:139
  872.6 4.9 copy-start.15
  885.4 5.1 copy-start.51
  917.0 4.6 collective-permute-start.1
  959.9 100.7 %collective-permute-start = (bf16[128,512]{1,0:T(8,128)(2,1)}, bf16[128,512]{1,0:T(8,128)(2,1)}, u32[]{:S(2)}, u32[]{:S(2)}) collective-permute-start(bf16[128,512]{1,0:T(8,128)(2,1)} %get-tuple-element.1072), channel_id=1, source_target_pairs={{0,64},{1,65},{2,66},{3,67},{4,68},{5,69},{6,70},{7,71},{8,72},{9,... | collective-permute-start | bytes 393224 | tf_op jit(solution)/shard_map/while/body/eval_jaxpr/ppermute | solution.py:139
  1025.4 5.1 copy-start.51
  1057.0 4.6 collective-permute-start.1
  1099.9 100.7 %collective-permute-start = (bf16[128,512]{1,0:T(8,128)(2,1)}, bf16[128,512]{1,0:T(8,128)(2,1)}, u32[]{:S(2)}, u32[]{:S(2)}) collective-permute-start(bf16[128,512]{1,0:T(8,128)(2,1)} %get-tuple-element.1072), channel_id=1, source_target_pairs={{0,64},{1,65},{2,66},{3,67},{4,68},{5,69},{6,70},{7,71},{8,72},{9,... | collective-permute-start | bytes 393224 | tf_op jit(solution)/shard_map/while/body/eval_jaxpr/ppermute | solution.py:139
  1165.5 5.1 copy-start.51
  1197.0 4.6 collective-permute-start.1
  1240.0 100.7 %collective-permute-start = (bf16[128,512]{1,0:T(8,128)(2,1)}, bf16[128,512]{1,0:T(8,128)(2,1)}, u32[]{:S(2)}, u32[]{:S(2)}) collective-permute-start(bf16[128,512]{1,0:T(8,128)(2,1)} %get-tuple-element.1072), channel_id=1, source_target_pairs={{0,64},{1,65},{2,66},{3,67},{4,68},{5,69},{6,70},{7,71},{8,72},{9,... | collective-permute-start | bytes 393224 | tf_op jit(solution)/shard_map/while/body/eval_jaxpr/ppermute | solution.py:139
  1305.5 5.1 copy-start.51
  1337.1 4.6 collective-permute-start.1
  1380.0 100.7 %collective-permute-start = (bf16[128,512]{1,0:T(8,128)(2,1)}, bf16[128,512]{1,0:T(8,128)(2,1)}, u32[]{:S(2)}, u32[]{:S(2)}) collective-permute-start(bf16[128,512]{1,0:T(8,128)(2,1)} %get-tuple-element.1072), channel_id=1, source_target_pairs={{0,64},{1,65},{2,66},{3,67},{4,68},{5,69},{6,70},{7,71},{8,72},{9,... | collective-permute-start | bytes 393224 | tf_op jit(solution)/shard_map/while/body/eval_jaxpr/ppermute | solution.py:139
  1445.5 5.1 copy-start.51
  1477.1 4.6 collective-permute-start.1
  1520.0 100.7 %collective-permute-start = (bf16[128,512]{1,0:T(8,128)(2,1)}, bf16[128,512]{1,0:T(8,128)(2,1)}, u32[]{:S(2)}, u32[]{:S(2)}) collective-permute-start(bf16[128,512]{1,0:T(8,128)(2,1)} %get-tuple-element.1072), channel_id=1, source_target_pairs={{0,64},{1,65},{2,66},{3,67},{4,68},{5,69},{6,70},{7,71},{8,72},{9,... | collective-permute-start | bytes 393224 | tf_op jit(solution)/shard_map/while/body/eval_jaxpr/ppermute | solution.py:139
  1585.6 5.1 copy-start.51
  1617.1 4.6 collective-permute-start.1
  1660.0 100.7 %collective-permute-start = (bf16[128,512]{1,0:T(8,128)(2,1)}, bf16[128,512]{1,0:T(8,128)(2,1)}, u32[]{:S(2)}, u32[]{:S(2)}) collective-permute-start(bf16[128,512]{1,0:T(8,128)(2,1)} %get-tuple-element.1072), channel_id=1, source_target_pairs={{0,64},{1,65},{2,66},{3,67},{4,68},{5,69},{6,70},{7,71},{8,72},{9,... | collective-permute-start | bytes 393224 | tf_op jit(solution)/shard_map/while/body/eval_jaxpr/ppermute | solution.py:139
  1725.6 5.1 copy-start.51
  1757.1 4.6 collective-permute-start.1
  1763.5 100.7 %collective-permute-start = (bf16[128,512]{1,0:T(8,128)(2,1)}, bf16[128,512]{1,0:T(8,128)(2,1)}, u32[]{:S(2)}, u32[]{:S(2)}) collective-permute-start(bf16[128,512]{1,0:T(8,128)(2,1)} %get-tuple-element.1072), channel_id=1, source_target_pairs={{0,64},{1,65},{2,66},{3,67},{4,68},{5,69},{6,70},{7,71},{8,72},{9,... | collective-permute-start | bytes 393224 | tf_op jit(solution)/shard_map/while/body/eval_jaxpr/ppermute | solution.py:139
  1765.4 99.7 %collective-permute-start.1 = (bf16[128,512]{1,0:T(8,128)(2,1)}, bf16[128,512]{1,0:T(8,128)(2,1)S(1)}, u32[]{:S(2)}, u32[]{:S(2)}) collective-permute-start(bf16[128,512]{1,0:T(8,128)(2,1)} %get-tuple-element.1075), channel_id=1, source_target_pairs={{64,0},{65,1},{66,2},{67,3},{68,4},{69,5},{70,6},{71,7},{72,8},{73... | collective-permute-start | bytes 393224 | tf_op jit(solution)/shard_map/while/body/eval_jaxpr/ppermute | solution.py:140
  1867.8 312.1 %reduce-scatter.7.cloned.1.call-start = ((), (), s32[]{:S(2)}) async-start(), calls=%async_computation.6 | async-start | bytes 2129920 | tf_op jit(solution)/shard_map/reduce_scatter | solution.py:156
  1871.1 583.7 %reduce-scatter.5.cloned.1.call-start = ((), (), s32[]{:S(2)}) async-start(), calls=%async_computation.5 | async-start | bytes 6389760 | tf_op jit(solution)/shard_map/reduce_scatter | solution.py:156
  1876.2 903.2 %reduce-scatter.9.cloned.1.call-start = ((), (), s32[]{:S(2)}) async-start(), calls=%async_computation.7 | async-start | bytes 8519680 | tf_op jit(solution)/shard_map/reduce_scatter | solution.py:156
  1884.1 1261.9 %reduce-scatter.11.cloned.1.call-start = ((), (), s32[]{:S(2)}) async-start(), calls=%async_computation.8 | async-start | bytes 8519680 | tf_op jit(solution)/shard_map/reduce_scatter | solution.py:156
  (684 other events, 1806.2 us)
Sparse Core Ops, SparseCore 0:
  1868.0 27.6 all-reduce.1
Sparse Core Ops, SparseCore 1:
  1871.2 308.6 reduce-scatter.6
  2184.8 269.9 reduce-scatter.4
  2457.6 321.7 reduce-scatter.8
  2782.4 363.6 reduce-scatter.10
where the time goes:
time: 3220 us; the launch traced here: 3160 us
  waiting for transfers between devices  1270 us (39%)
  matrix products  1020 us (32%)
  local copies, waits for them, and re-layouts  538 us (17%)
  starting transfers between devices  198 us (6%)
  other arithmetic  104 us (3%)
    reduce_scatter x4, waiting for transfers between devices, device_step(): lax.psum_scatter(jnp.stack([grad_accs[layer_idx][weight_idx] for layer_id...  1250 us
    cond x1396, local copies, waits for them, and re-layouts  228 us
    ppermute x14, starting transfers between devices, tick(): recv_bwd = lax.ppermute(send_bwd, 'pp', bwd_pairs)  180 us
    slice x96, local copies, waits for them, and re-layouts, layer_forward(): k_heads = qkv_act[:, model_width:2 * model_width].reshape(head_shape)  107 us
    sub x48, matrix products, causal_probs(): return jax.nn.softmax(jnp.where(allowed, scores, -1e+30), axis=-1)  104 us
    dot_general x48, matrix products, layer_forward(): jnp.einsum('bhqk,bkhe->bqhe', attn_probs.astype(jnp.bfloat16), v_heads, p...  96.7 us
    dot_general x24, matrix products, layer_forward(): jnp.dot(c_norm, w_up, preferred_element_type=jnp.float32)  95.1 us
    dot_general x24, matrix products, layer_forward(): jnp.dot(gelu_act, w_down, preferred_element_type=jnp.float32)  93.9 us
  transfers between devices with their start and end apart: 33, of which 19 were waited for; matrix products, arithmetic and copies ran while one was open for 30% of the time, Pallas kernels for 0%

commit v1 on v0

v1 whole, which is shorter than its diff:
```python
import functools
import math

import jax
import jax.numpy as jnp
from jax import lax
from jax.experimental import pallas as pl
from jax.experimental.pallas import tpu as pltpu
from jax.sharding import PartitionSpec as P

F32 = jnp.float32
BF16 = jnp.bfloat16
MESH = pl.DeviceIdType.MESH

D = 512
HD = 64
LN = 128
TILE = (8, LN)
NU = 6
SEQ = LN
NSEQ = 6
ROWS = NSEQ * SEQ
LAYERS = 4
EPS = 1e-6
GELU_C1 = math.sqrt(2.0 / math.pi)
GELU_C2 = GELU_C1 * 0.044715
EXP2_SCALE = HD ** -0.5 * math.log2(math.e)
W_SHAPES = ((D, 3 * D), (D, D), (D, 4 * D), (4 * D, D))
LAST = (((1,), (1,)), ((), ()))
FIRST = (((0,), (0,)), ((), ()))


def dot(a, b):
    return jnp.dot(a, b, preferred_element_type=F32)


def dot_last(a, b):
    return lax.dot_general(a, b, LAST, preferred_element_type=F32)


def dot_first(a, b):
    return lax.dot_general(a, b, FIRST, preferred_element_type=F32)


def inv_rms(h):
    return lax.rsqrt(jnp.mean(h * h, axis=-1, keepdims=True) + EPS)


def rms_bwd(h, g):
    ir = inv_rms(h)
    n = h * ir
    return ir * (g - n * jnp.mean(g * n, axis=-1, keepdims=True))


def gelu(u):
    t = jnp.tanh(u * (GELU_C1 + GELU_C2 * (u * u)))
    hu = 0.5 * u
    return hu + hu * t


def gelu_and_slope(u):
    a = GELU_C2 * (u * u)
    t = jnp.tanh(u * (a + GELU_C1))
    hu = 0.5 * u
    ht = hu * t
    return hu + ht, (0.5 * t + 0.5) + (hu - ht * t) * (3.0 * a + GELU_C1)


def block_diag(x):
    first = lax.broadcasted_iota(jnp.int32, (SEQ, 2 * HD), 1) < HD
    zero = jnp.zeros_like(x)
    return jnp.concatenate([jnp.where(first, x, zero), jnp.where(first, zero, x)], axis=0)


def units_of(step, n_seqs):
    return [(pl.ds(pl.multiple_of((step * n_seqs + n) * SEQ, SEQ), SEQ), pair) for n in range(n_seqs) for pair in range(4)]


def attention_fwd(step, n_seqs, qkv, p_out, o_out):
    key = lax.broadcasted_iota(jnp.int32, (SEQ, SEQ), 0)
    query = lax.broadcasted_iota(jnp.int32, (SEQ, SEQ), 1)
    allowed = key <= query
    units = units_of(step, n_seqs)

    def scores(rows, pair):
        c = pair * LN
        return dot_last(qkv[rows, D + c:D + c + LN], block_diag(qkv[rows, c:c + LN]))

    ahead = 2
    pending = [scores(*u) for u in units[:ahead]]
    for i, (rows, pair) in enumerate(units):
        if i + ahead < len(units):
            pending.append(scores(*units[i + ahead]))
        s = pending[i]
        c = pair * LN
        probs = []
        for head in range(2):
            sh = jnp.where(allowed, s[:, head * LN:head * LN + LN], -1e30)
            e = jnp.exp2((sh - jnp.max(sh, axis=0, keepdims=True)) * EXP2_SCALE)
            p = e * (1.0 / jnp.sum(e, axis=0, keepdims=True))
            p_out[rows, 2 * c + head * LN:2 * c + head * LN + LN] = p
            probs.append(p.astype(BF16))
        v = qkv[rows, 2 * D + c:2 * D + c + LN]
        o_out[rows, c:c + LN] = dot_first(jnp.concatenate(probs, axis=0), block_diag(v)).astype(BF16)


def attention_bwd(step, n_seqs, qkv, p_in, do):
    units = units_of(step, n_seqs)

    def first(rows, pair):
        c = pair * LN
        d = block_diag(do[rows, c:c + LN])
        return d, dot_last(qkv[rows, 2 * D + c:2 * D + c + LN], d)

    ahead = 2
    pending = [first(*u) for u in units[:ahead]]
    for i, (rows, pair) in enumerate(units):
        if i + ahead < len(units):
            pending.append(first(*units[i + ahead]))
        d, dp = pending[i]
        c = pair * LN
        q = qkv[rows, c:c + LN]
        k = qkv[rows, D + c:D + c + LN]
        p = p_in[rows, 2 * c:2 * c + 256]
        dv = dot(p.astype(BF16), d).astype(BF16)
        pd = p * dp
        ds = ((pd - p * jnp.sum(pd, axis=0, keepdims=True)) * HD ** -0.5).astype(BF16)
        dk = dot(ds, block_diag(q)).astype(BF16)
        dq = dot_first(jnp.concatenate([ds[:, :LN], ds[:, LN:]], axis=0), block_diag(k)).astype(BF16)
        qkv[rows, c:c + LN] = dq
        qkv[rows, D + c:D + c + LN] = dk
        qkv[rows, 2 * D + c:2 * D + c + LN] = dv


AXES = (("x", "y", "z"), ("y", "z", "x"), ("z", "x", "y"))
NAT = ("z", "y", "x")
STRIDE = {"x": 1, "y": 4, "z": 16}
UNITS = [(colour, way) for colour in range(3) for way in (1, -1)]


class Place:
    def __init__(self):
        self.core = lax.axis_index("pp")
        self.dp = lax.axis_index("dp")
        self.at = {"x": lax.rem(self.dp, 4), "y": lax.rem(self.dp // 4, 4), "z": self.dp // 16}

    def neighbour(self, axis, way):
        c = self.at[axis]
        return (self.core, self.dp + (lax.rem(c + way + 4, 4) - c) * STRIDE[axis])

    def partner(self):
        return (1 - self.core, self.dp)

    def block(self, axis, way, step):
        return lax.rem(self.at[axis] - way * (1 + step) + 8, 4)


def greet(peers):
    barrier = pltpu.get_barrier_semaphore()
    for p in peers:
        pl.semaphore_signal(barrier, inc=1, device_id=p, device_id_type=MESH)
    pl.semaphore_wait(barrier, len(peers))


FWD_SEQS = 3


def forward_kernel(x, wq, wo, wu, wd, y, rq, ro, ru, rd, hs, qs, ps, os, ms, us,
                   h, qkv, p, o, m, u, vq, vo, vu, vd, wsem, psem, qsem, osem, ysem, hsem):
    place = Place()
    core = place.core
    mine = (wq, wo, wu, wd)
    theirs = (rq, ro, ru, rd)
    held = (vq, vo, vu, vd)

    def push(k, j):
        return pltpu.make_async_remote_copy(mine[k].at[j], theirs[k].at[j], psem.at[k, j], qsem.at[k, j],
                                            device_id=place.partner(), device_id_type=MESH)

    def fetch(k, l):
        local = lax.rem(l, 2)

        @pl.when(l // 2 == core)
        def _():
            pltpu.make_async_copy(mine[k].at[local], held[k].at[local], wsem.at[k, local]).start()

        @pl.when(l // 2 != core)
        def _():
            push(k, local).wait_recv()
            pltpu.make_async_copy(theirs[k].at[local], held[k].at[local], wsem.at[k, local]).start()

    def weight(k, l):
        local = lax.rem(l, 2)
        pltpu.make_async_copy(mine[k].at[0], held[k].at[local], wsem.at[k, local]).wait()
        return held[k].at[local]

    saved = ((h, hs), (qkv, qs), (p, ps), (o, os), (m, ms), (u, us))

    def save(i, l):
        src, dst = saved[i]
        return pltpu.make_async_copy(src.at[lax.rem(l, 2)] if i == 0 else src, dst.at[l], osem.at[i])

    first = pltpu.make_async_copy(x.at[pl.ds(core * ROWS, ROWS)], h.at[0], hsem)
    first.start()
    greet([place.partner()])
    for j in range(2):
        for k in range(4):
            push(k, j).start()
    fetch(0, 0)
    fetch(1, 0)
    first.wait()

    def layer(l, _):
        now, later = lax.rem(l, 2), lax.rem(l + 1, 2)

        def again(i):
            @pl.when(l > 0)
            def _():
                save(i, l - 1).wait()

        w = weight(0, l)
        hf = h[now].astype(F32)
        a = (hf * inv_rms(hf)).astype(BF16)
        again(0)
        save(0, l).start()
        again(1)
        qkv[...] = dot(a, w[...]).astype(BF16)
        save(1, l).start()
        again(2)
        again(3)

        def attend(i, _):
            attention_fwd(i, FWD_SEQS, qkv, p, o)
            return 0

        lax.fori_loop(0, NSEQ // FWD_SEQS, attend, 0)
        save(2, l).start()
        save(3, l).start()

        @pl.when(l == 0)
        def _():
            fetch(2, 0)
            fetch(3, 0)

        @pl.when(l < LAYERS - 1)
        def _():
            fetch(0, l + 1)
            fetch(1, l + 1)

        w = weight(1, l)
        again(4)
        mb = (h[now].astype(F32) + dot(o[...], w[...])).astype(BF16)
        m[...] = mb
        save(4, l).start()
        wup, wdn = weight(2, l), weight(3, l)
        again(5)
        mf = m[...].astype(F32)
        c = (mf * inv_rms(mf)).astype(BF16)
        acc = mf
        for j in range(2):
            cols = slice(j * 2 * D, (j + 1) * 2 * D)
            ub = dot(c, wup[:, cols]).astype(BF16)
            u[:, cols] = ub
            acc = acc + dot(gelu(ub.astype(F32)).astype(BF16), wdn[cols, :])
        h[later] = acc.astype(BF16)
        save(5, l).start()

        @pl.when(l < LAYERS - 1)
        def _():
            fetch(2, l + 1)
            fetch(3, l + 1)
        return 0

    lax.fori_loop(0, LAYERS, layer, 0)
    rows = pl.ds(core * ROWS, ROWS)
    out = pltpu.make_async_copy(h.at[0], y.at[rows], ysem.at[0])
    cross = pltpu.make_async_remote_copy(h.at[0], y.at[rows], ysem.at[1], ysem.at[2],
                                         device_id=place.partner(), device_id_type=MESH)
    out.start()
    cross.start()
    for i in range(NU):
        save(i, LAYERS - 1).wait()
    for j in range(2):
        for k in range(4):
            push(k, j).wait_send()
    out.wait()
    cross.wait_send()
    cross.wait_recv()


def forward(x, weights):
    act = lambda cols, dt=BF16: jax.ShapeDtypeStruct((LAYERS, ROWS, cols), dt)
    other = [jax.ShapeDtypeStruct((2,) + s, BF16) for s in W_SHAPES]
    anywhere = pl.BlockSpec(memory_space=pl.ANY)
    return pl.pallas_call(
        forward_kernel,
        name="forward",
        out_shape=[jax.ShapeDtypeStruct((2 * ROWS, D), BF16)] + other
        + [act(D), act(3 * D), act(2 * D, F32), act(D), act(D), act(4 * D)],
        in_specs=[anywhere] * 5,
        out_specs=[anywhere] * 11,
        scratch_shapes=[
            pltpu.VMEM((2, ROWS, D), BF16), pltpu.VMEM((ROWS, 3 * D), BF16), pltpu.VMEM((ROWS, 2 * D), F32),
            pltpu.VMEM((ROWS, D), BF16), pltpu.VMEM((ROWS, D), BF16), pltpu.VMEM((ROWS, 4 * D), BF16),
        ] + [pltpu.VMEM((2,) + s, BF16) for s in W_SHAPES] + [
            pltpu.SemaphoreType.DMA((4, 2)), pltpu.SemaphoreType.DMA((4, 2)), pltpu.SemaphoreType.DMA((4, 2)),
            pltpu.SemaphoreType.DMA((6,)), pltpu.SemaphoreType.DMA((3,)), pltpu.SemaphoreType.DMA,
        ],
        compiler_params=pltpu.CompilerParams(collective_id=1, has_side_effects=True, vmem_limit_bytes=60 * 2 ** 20),
    )(x, *weights)


CHUNKS = 16
STREAMS = 4
POS = {1: 0, 0: 1, 3: 2, 2: 3}
J0 = {1: 0, 0: 1, 3: 1, 2: 2}


def ring_scratch():
    return [
        pltpu.VMEM((STREAMS, 6, 4, 4, *TILE), F32), pltpu.VMEM((STREAMS, 2, 6, 4, 4, *TILE), F32),
        pltpu.VMEM((STREAMS, 6, 4, 4, *TILE), F32),
        pltpu.VMEM((STREAMS, 6, 4, *TILE), F32), pltpu.VMEM((STREAMS, 2, 6, 4, *TILE), F32),
        pltpu.VMEM((STREAMS, 6, 4, *TILE), F32),
        pltpu.VMEM((STREAMS, 6, *TILE), F32), pltpu.VMEM((STREAMS, 2, 6, *TILE), F32),
        pltpu.SemaphoreType.DMA((STREAMS, 3, 2, 6)), pltpu.SemaphoreType.DMA((STREAMS, 3, 2, 6)),
    ]


def pick_block(ref, axis, b):
    return {"z": lambda: ref[b], "y": lambda: ref[:, b], "x": lambda: ref[:, :, b]}[axis]()


class Rings:
    def __init__(self, place, scratch, own, ready, done):
        self.p, self.own, self.ready, self.done = place, own, ready, done
        (self.s1, self.r1, self.t1, self.s2, self.r2, self.t2, self.s3, self.r3, self.ss, self.rs) = scratch

    def copy(self, e, phase, par, u):
        colour, way = UNITS[u]
        src = (self.s1, self.s2, self.s3)[phase].at[e, u]
        dst = (self.r1, self.r2, self.r3)[phase].at[e, par, u]
        return pltpu.make_async_remote_copy(src, dst, self.ss.at[e, phase, par, u], self.rs.at[e, phase, par, u],
                                            device_id=self.p.neighbour(AXES[colour][phase], way), device_id_type=MESH)

    def wait(self, e, phase, par):
        for u in range(NU):
            c = self.copy(e, phase, par, u)
            c.wait_send()
            c.wait_recv()

    def send(self, e, phase, par):
        for u in range(NU):
            self.copy(e, phase, par, u).start()

    def block(self, u, phase, step):
        colour, way = UNITS[u]
        return self.p.block(AXES[colour][phase], way, step)

    def own_block(self, ref, u, step):
        return pick_block(ref.at[u], AXES[UNITS[u][0]][0], self.block(u, 0, step))

    def second(self, e, u, step):
        order = AXES[UNITS[u][0]]
        b = self.block(u, 1, step)
        rest = [a for a in NAT if a != order[0]]
        return self.t1[e, u, :, b] if rest.index(order[1]) == 1 else self.t1[e, u, b]

    def third(self, e, u, step):
        return self.t2[e, u, self.block(u, 2, step)]

    def slot(self, n, iteration):
        e, j = n % STREAMS, n // STREAMS
        step = (j - J0[e]) % 3
        k = iteration + (j - J0[e]) // 3
        tick = lax.rem(3 * iteration + j, 2)
        par, old = tick, 1 - tick
        chunk = lambda i: STREAMS * (k - i) + POS[e] - 1
        live = lambda i: (chunk(i) >= 0) & (chunk(i) < CHUNKS)
        if step == 0:
            @pl.when(live(3))
            def _():
                self.wait(e, 2, old)
                for u in range(NU):
                    self.done[chunk(3), u] = self.r3[e, old, u] + self.third(e, u, 3)

            @pl.when(live(2))
            def _():
                self.wait(e, 1, old)
                for u in range(NU):
                    self.t2[e, u] = self.r2[e, old, u] + self.second(e, u, 3)
                    self.s3[e, u] = self.third(e, u, 0)

            @pl.when(live(1))
            def _():
                self.wait(e, 0, old)
                own = self.own(chunk(1))
                for u in range(NU):
                    self.t1[e, u] = self.r1[e, old, u] + self.own_block(own, u, 3)
                    self.s2[e, u] = self.second(e, u, 0)

            @pl.when(live(0))
            def _():
                self.ready(chunk(0))
                own = self.own(chunk(0))
                for u in range(NU):
                    self.s1[e, u] = self.own_block(own, u, 0)
        else:
            @pl.when(live(2))
            def _():
                self.wait(e, 2, old)
                for u in range(NU):
                    self.s3[e, u] = self.r3[e, old, u] + self.third(e, u, step)

            @pl.when(live(1))
            def _():
                self.wait(e, 1, old)
                for u in range(NU):
                    self.s2[e, u] = self.r2[e, old, u] + self.second(e, u, step)

            @pl.when(live(0))
            def _():
                self.wait(e, 0, old)
                own = self.own(chunk(0))
                for u in range(NU):
                    self.s1[e, u] = self.r1[e, old, u] + self.own_block(own, u, step)
        for phase in range(3):
            @pl.when(live(phase))
            def _():
                self.send(e, phase, par)


def tiles_of_layer():
    down = [(3, g, j) for j in range(4) for g in range(4)]
    up = [(2, 0, j) for j in range(16)]
    out = [(1, 0, j) for j in range(4)]
    qkv = [(0, 0, j) for j in range(12)]
    return down + up + out + qkv


TILES = tiles_of_layer()
PLACE_OF = {t: (i // 12, i % 12 // 6, i % 6) for i, t in enumerate(TILES)}


BWD_SEQS = 2
OWN_SLOTS = 8
DRAIN = 4


def backward_kernel(seed, wq, wo, wu, wd, rq, ro, ru, rd, hs, qs, ps, os, ms, us,
                    gq, go, gu, gd,
                    grads, recv, done, done_rx, h, qkv, p, o, m, u, e, g, g1, do, vq, vo, vu, vd,
                    wsem, asem, gsem, dsend, drecv, fsem, credit, *ring):
    place = Place()
    core = place.core
    mine = (wq, wo, wu, wd)
    theirs = (rq, ro, ru, rd)
    held = (vq, vo, vu, vd)
    acts = ((h, hs), (qkv, qs), (p, ps), (o, os), (m, ms), (u, us))
    H, QKV, PROB, O, M, U = range(6)

    def fetch_w(k, l):
        for c in range(2):
            src = (mine if c == 0 else theirs)[k]

            @pl.when((l // 2 == core) if c == 0 else (l // 2 != core))
            def _():
                pltpu.make_async_copy(src.at[lax.rem(l, 2)], held[k], wsem.at[k]).start()

    def wait_w(k):
        pltpu.make_async_copy(mine[k].at[0], held[k], wsem.at[k]).wait()

    def act(i, l):
        dst, src = acts[i]
        return pltpu.make_async_copy(src.at[l], dst, asem.at[i])

    def own_slot(chunk):
        return lax.rem(chunk, OWN_SLOTS)

    def cross(chunk):
        q = lax.rem(chunk, 4)
        return pltpu.make_async_remote_copy(grads.at[OWN_SLOTS + q], recv.at[q], dsend.at[q], drecv.at[q],
                                            device_id=place.partner(), device_id_type=MESH)

    def ready(chunk):
        q = lax.rem(chunk, 4)
        cross(chunk).wait_recv()
        for unit in range(NU):
            grads[own_slot(chunk), unit] = grads[own_slot(chunk), unit] + recv[q, unit]

        @pl.when(chunk + 4 < CHUNKS)
        def _():
            pl.semaphore_signal(credit.at[q], inc=1, device_id=place.partner(), device_id_type=MESH)

    rings = Rings(place, ring, lambda chunk: grads.at[own_slot(chunk)], ready, done)

    seed_in = pltpu.make_async_copy(seed.at[pl.ds(core * ROWS, ROWS)], g, gsem)
    seed_in.start()
    for k in (3, 2):
        fetch_w(k, LAYERS - 1)
    for i in (U, M, O, PROB, QKV, H):
        act(i, LAYERS - 1).start()
    for k in (1, 0):
        fetch_w(k, LAYERS - 1)
    greet([place.partner()] + [place.neighbour(a, way) for a in NAT for way in (1, -1)])
    seed_in.wait()

    def iteration(it, _):
        l = LAYERS - 1 - it
        busy = it < LAYERS
        more = it < LAYERS - 1
        base = 4 * it

        def free(q):
            @pl.when(it > 0)
            def _():
                cross(base - 4 + q).wait_send()

        def put(array, row_group, col, value):
            q, half, unit = PLACE_OF[array, row_group, col]
            index = jnp.where(core == half, own_slot(base + q), OWN_SLOTS + q)
            grads[index, unit] = value.reshape(4, 4, 4, *TILE)

        def ship(q):
            @pl.when(it > 0)
            def _():
                pl.semaphore_wait(credit.at[q], 1)
            cross(base + q).start()

        def gelu_part(j):
            cols = slice(j * D, (j + 1) * D)
            de = dot_last(g[...], vd[cols, :])
            ej, slope = gelu_and_slope(u[:, cols].astype(F32))
            e[:, cols] = ej.astype(BF16)
            u[:, cols] = (slope * de).astype(BF16)

        def piece(n):
            if n == 0:
                wait_w(3)
                act(U, l).wait()
                gelu_part(0)
                gelu_part(1)
            elif n == 1:
                gelu_part(2)
                gelu_part(3)

                @pl.when(more)
                def _():
                    fetch_w(3, l - 1)
            elif n == 2:
                free(0)
                free(1)
                for half in range(2):
                    w = dot_first(e[...], g[:, half * 256:half * 256 + 256]).reshape(64, 4, 8, 256)
                    for j in range(2):
                        for rg in range(4):
                            put(3, rg, 2 * half + j, w[:, rg, :, j * LN:j * LN + LN])
                ship(0)
            elif n == 3:
                wait_w(2)
                act(M, l).wait()
                dc = dot_last(u[...], vu[...])
                g1[...] = (g[...].astype(F32) + rms_bwd(m[...].astype(F32), dc)).astype(BF16)

                @pl.when(more)
                def _():
                    fetch_w(2, l - 1)
            elif n == 4:
                free(2)
                mf = m[...].astype(F32)
                c = (mf * inv_rms(mf)).astype(BF16)
                for part in range(4):
                    w = dot_first(c, u[:, part * D:part * D + D]).reshape(64, 8, D)
                    for j in range(4):
                        put(2, 0, 4 * part + j, w[:, :, j * LN:j * LN + LN])
                ship(1)

                @pl.when(more)
                def _():
                    act(U, l - 1).start()
                    act(M, l - 1).start()
            elif n == 5:
                wait_w(1)
                act(O, l).wait()
                do[...] = dot_last(g1[...], vo[...]).astype(BF16)
                w = dot_first(o[...], g1[...]).reshape(64, 8, D)
                for j in range(4):
                    put(1, 0, j, w[:, :, j * LN:j * LN + LN])
                ship(2)

                @pl.when(more)
                def _():
                    fetch_w(1, l - 1)
                    act(O, l - 1).start()
            elif n in (6, 7, 8):
                if n == 6:
                    act(PROB, l).wait()
                    act(QKV, l).wait()
                attention_bwd(n - 6, BWD_SEQS, qkv, p, do)
                if n == 8:
                    @pl.when(more)
                    def _():
                        act(PROB, l - 1).start()
            elif n == 9:
                wait_w(0)
                act(H, l).wait()
                da = dot_last(qkv[...], vq[...])
                g[...] = (g1[...].astype(F32) + rms_bwd(h[...].astype(F32), da)).astype(BF16)

                @pl.when(more)
                def _():
                    fetch_w(0, l - 1)
            elif n == 10:
                free(3)
                hf = h[...].astype(F32)
                a = (hf * inv_rms(hf)).astype(BF16)
                for part in range(3):
                    w = dot_first(a, qkv[:, part * D:part * D + D]).reshape(64, 8, D)
                    for j in range(4):
                        put(0, 0, 4 * part + j, w[:, :, j * LN:j * LN + LN])
                ship(3)

                @pl.when(more)
                def _():
                    act(H, l - 1).start()
                    act(QKV, l - 1).start()

        for n in range(12):
            if n < 11:
                @pl.when(busy)
                def _():
                    piece(n)
            rings.slot(n, it)
        return 0

    lax.fori_loop(0, LAYERS + DRAIN, iteration, 0)
    for q in range(4):
        cross(CHUNKS - 4 + q).wait_send()

    kept = 8 * (1 - core)
    last = pltpu.make_async_remote_copy(done.at[pl.ds(8 * core, 8)], done_rx, fsem.at[0], fsem.at[1],
                                        device_id=place.partner(), device_id_type=MESH)
    last.start()
    last.wait_send()
    last.wait_recv()
    outs = (gq, go, gu, gd)
    for layer in range(2):
        for tile in TILES:
            array, rg, col = tile
            q, half, unit = PLACE_OF[tile]
            i = 4 * (1 - layer) + q
            value = jnp.where(core == half, done[kept + i, unit], done_rx[i, unit])
            outs[array][layer, rg * 8:rg * 8 + 8, col * LN:col * LN + LN] = value


def backward(seed, weights, saved):
    anywhere = pl.BlockSpec(memory_space=pl.ANY)
    vmem = pl.BlockSpec(memory_space=pltpu.VMEM)
    act = lambda cols, dt=BF16: pltpu.VMEM((ROWS, cols), dt)
    return pl.pallas_call(
        backward_kernel,
        name="backward",
        out_shape=[jax.ShapeDtypeStruct(s, F32) for s in ((2, 8, 3 * D), (2, 8, D), (2, 8, 4 * D), (2, 32, D))],
        in_specs=[anywhere] * 15,
        out_specs=[vmem] * 4,
        scratch_shapes=[
            pltpu.VMEM((OWN_SLOTS + 4, 6, 4, 4, 4, *TILE), F32),
            pltpu.VMEM((4, 6, 4, 4, 4, *TILE), F32),
            pltpu.VMEM((CHUNKS, 6, *TILE), F32), pltpu.VMEM((8, 6, *TILE), F32),
            act(D), act(3 * D), act(2 * D, F32), act(D), act(D), act(4 * D), act(4 * D), act(D), act(D), act(D),
        ] + [pltpu.VMEM(s, BF16) for s in W_SHAPES] + [
            pltpu.SemaphoreType.DMA((4,)), pltpu.SemaphoreType.DMA((6,)), pltpu.SemaphoreType.DMA,
            pltpu.SemaphoreType.DMA((4,)), pltpu.SemaphoreType.DMA((4,)), pltpu.SemaphoreType.DMA((2,)),
            pltpu.SemaphoreType.REGULAR((4,)),
        ] + ring_scratch(),
        compiler_params=pltpu.CompilerParams(collective_id=2, has_side_effects=True, vmem_limit_bytes=67043328),
    )(seed, *weights, *saved)


def solution(mesh):
    def step(x_in, seed_grad, w_qkv, w_out, w_up, w_down):
        shape = x_in.shape
        weights = (w_qkv, w_out, w_up, w_down)
        y, *saved = forward(x_in.reshape(2 * ROWS, D), weights)
        gq, go, gu, gd = backward(seed_grad.reshape(2 * ROWS, D), weights, saved)
        return y.reshape(shape), gq, go, gu, gd

    act, weight, grad = P(None, "dp"), P("pp"), P("pp", "dp")
    return jax.shard_map(
        step,
        mesh=mesh,
        in_specs=(act, act, weight, weight, weight, weight),
        out_specs=(act, grad, grad, grad, grad),
        check_vma=False,
    )
```

time: 3220 us -> 201 us (0.06); the launches traced: 3160 us -> 201 us
  waiting for transfers between devices: 1270 us -> 0 us
  matrix products: 1020 us -> 0 us
  local copies, waits for them, and re-layouts: 538 us -> 5.29 us
  starting transfers between devices: 198 us -> 0 us
  Pallas kernels: 0 us -> 195 us
  other arithmetic: 104 us -> 0 us
    reduce_scatter x4 -> x0, waiting for transfers between devices: 1250 us -> none  [device_step(): lax.psum_scatter(jnp.stack([grad_accs[layer_idx][weight_idx] for layer_id...]
    dot_general x504 -> x0, matrix products: 919 us -> none  [the longest x48 96.7 us: layer_forward(): jnp.einsum('bhqk,bkhe->bqhe', attn_probs.astype(jnp.bfloat16), v_heads, p...]
    slice x192 -> x0, local copies, waits for them, and re-layouts: 238 us -> none  [the longest x96 107 us: layer_forward(): k_heads = qkv_act[:, model_width:2 * model_width].reshape(head_shape)]
    cond x1396 -> x0, local copies, waits for them, and re-layouts: 228 us -> none
    ppermute x28 -> x0, starting transfers between devices: 198 us -> none  [the longest x14 180 us: tick(): recv_bwd = lax.ppermute(send_bwd, 'pp', bwd_pairs)]
    pallas_call x0 -> x2, Pallas kernels: none -> 195 us  [the longest x1 148 us: backward(): pl.pallas_call(backward_kernel, name='backward', out_shape=[jax.ShapeDtyp...]
    sub x48 -> x0, matrix products: 104 us -> none  [causal_probs(): return jax.nn.softmax(jnp.where(allowed, scores, -1e+30), axis=-1)]
    convert_element_type x24 -> x0, local copies, waits for them, and re-layouts: 39.7 us -> none  [layer_input_grad(): lax.dot_general(d_mid, w_out, CONTRACT_COLS, preferred_element_type=jnp.f...]
  transfers between devices with their start and end apart: 33 -> 0, of which waited for: 19 -> 0; matrix products, arithmetic and copies ran while one was open for 30% -> 0% of each run, Pallas kernels for 0% -> 0%
where the time goes in v1:
time: 201 us
  Pallas kernels  195 us (97%)
  local copies, waits for them, and re-layouts  5.29 us (3%)
    pallas_call x1, Pallas kernels, backward(): pl.pallas_call(backward_kernel, name='backward', out_shape=[jax.ShapeDtyp...  148 us
    pallas_call x1, Pallas kernels, forward(): pl.pallas_call(forward_kernel, name='forward', out_shape=[jax.ShapeDtypeS...  47.1 us
    unnamed x13, local copies, waits for them, and re-layouts  5.29 us

profile of v1, /device:TPU:1, one launch (start us, length us, event | category | flops | bytes accessed | tf_op | source)
XLA Modules:
  0.0 201.0 jit_solution(17539852479930855361)
XLA Ops:
  0.6 47.1 %forward.1 = (bf16[1536,512]{1,0:T(8,128)(2,1)}, bf16[2,512,1536]{2,1,0:T(8,128)(2,1)}, bf16[2,512,512]{2,1,0:T(8,128)(2,1)}, bf16[2,512,2048]{2,1,0:T(8,128)(2,...) custom-call(bf16[1536,512]{1,0:T(8,128)(2,1)} %bitcast.5, ...), custom_call_target="tpu_custom_call" | custom-call | tf_op jit(solution)/shard_map/forward/pallas_call | solution.py:295
  47.7 148.0 %backward.1 = (f32[2,8,1536]{2,1,0:T(8,128)}, f32[2,8,512]{2,1,0:T(8,128)}, f32[2,8,2048]{2,1,0:T(8,128)}, f32[2,32,512]{2,1,0:T(8,128)}) custom-call(bf16[1536,512]{1,0:T(8,128)(2,1)} %bitcast.7, bf16[2,512,1536]{2,1,0:T(8,128)(2,1)} %wq.3, bf16[2,512,512]{2,1,0:T(8,128)(2,1)} %wo.3, bf16[2,512,2048]{2,1,0:T(8,128)(2,1)} %wu.3, bf16[2,2048,512]{2,1,0:T(8,128)(2,1)} %wd.3, ...), custom_call_target="tpu_custom_call" | custom-call | tf_op jit(solution)/shard_map/backward/pallas_call | solution.py:660
  195.7 0.0 copy-start.2
  195.7 0.0 copy-start.3
  195.7 0.0 copy-start.1
  195.7 0.0 copy-start
  195.7 2.7 %copy.17 = bf16[12,1,128,512]{3,2,1,0:T(8,128)(2,1)} copy(bf16[12,1,128,512]{3,2,1,0:T(8,128)(2,1)} %bitcast.6) | data formatting | bytes 3145728
  198.4 0.0 copy-done.2
  198.4 0.6 copy.18
  199.1 0.0 copy-done.3
  199.1 0.6 copy.19
  199.7 0.0 copy-done.1
  199.7 0.7 copy.20
  200.4 0.0 copy-done
  200.4 0.7 copy.21
Async XLA Ops:
  195.7 2.8 %copy-start.2 = (f32[2,8,1536]{2,1,0:T(8,128)S(1)}, f32[2,8,1536]{2,1,0:T(8,128)}, u32[]{:S(2)}) copy-start(f32[2,8,1536]{2,1,0:T(8,128)} %get-tuple-element.46) | copy-start | bytes 294916
  195.7 3.4 %copy-start.3 = (f32[2,8,512]{2,1,0:T(8,128)S(1)}, f32[2,8,512]{2,1,0:T(8,128)}, u32[]{:S(2)}) copy-start(f32[2,8,512]{2,1,0:T(8,128)} %get-tuple-element.47) | copy-start | bytes 98308
  195.7 4.0 %copy-start.1 = (f32[2,8,2048]{2,1,0:T(8,128)S(1)}, f32[2,8,2048]{2,1,0:T(8,128)}, u32[]{:S(2)}) copy-start(f32[2,8,2048]{2,1,0:T(8,128)} %get-tuple-element.48) | copy-start | bytes 393220
  195.7 4.6 %copy-start = (f32[2,32,512]{2,1,0:T(8,128)S(1)}, f32[2,32,512]{2,1,0:T(8,128)}, u32[]{:S(2)}) copy-start(f32[2,32,512]{2,1,0:T(8,128)} %get-tuple-element.49) | copy-start | bytes 393220

commit v2 on v1

v2 whole, which is shorter than its diff:
```python
import functools
import math

import jax
import jax.numpy as jnp
from jax import lax
from jax.experimental import pallas as pl
from jax.experimental.pallas import tpu as pltpu
from jax.sharding import PartitionSpec as P

F32 = jnp.float32
BF16 = jnp.bfloat16
MESH = pl.DeviceIdType.MESH

D = 512
HD = 64
LN = 128
TILE = (8, LN)
NU = 6
SEQ = LN
NSEQ = 6
ROWS = NSEQ * SEQ
LAYERS = 4
EPS = 1e-6
GELU_C1 = math.sqrt(2.0 / math.pi)
GELU_C2 = GELU_C1 * 0.044715
EXP2_SCALE = HD ** -0.5 * math.log2(math.e)
W_SHAPES = ((D, 3 * D), (D, D), (D, 4 * D), (4 * D, D))
LAST = (((1,), (1,)), ((), ()))
FIRST = (((0,), (0,)), ((), ()))


def dot(a, b):
    return jnp.dot(a, b, preferred_element_type=F32)


def dot_last(a, b):
    return lax.dot_general(a, b, LAST, preferred_element_type=F32)


def dot_first(a, b):
    return lax.dot_general(a, b, FIRST, preferred_element_type=F32)


def inv_rms(h):
    return lax.rsqrt(jnp.mean(h * h, axis=-1, keepdims=True) + EPS)


def rms_bwd(h, g):
    ir = inv_rms(h)
    n = h * ir
    return ir * (g - n * jnp.mean(g * n, axis=-1, keepdims=True))


def gelu(u):
    t = jnp.tanh(u * (GELU_C1 + GELU_C2 * (u * u)))
    return u * (0.5 * t + 0.5)


def gelu_and_slope(u):
    a = GELU_C2 * (u * u)
    t = jnp.tanh(u * (a + GELU_C1))
    half = 0.5 * t + 0.5
    e = u * half
    return e, half + e * (1.0 - t) * (3.0 * a + GELU_C1)


def block_diag(x):
    first = lax.broadcasted_iota(jnp.int32, (SEQ, 2 * HD), 1) < HD
    zero = jnp.zeros_like(x)
    return jnp.concatenate([jnp.where(first, x, zero), jnp.where(first, zero, x)], axis=0)


def units_of(step, n_seqs):
    return [(pl.ds(pl.multiple_of((step * n_seqs + n) * SEQ, SEQ), SEQ), pair) for n in range(n_seqs) for pair in range(4)]


def attention_fwd(step, n_seqs, qkv, p_out, o_out):
    key = lax.broadcasted_iota(jnp.int32, (SEQ, SEQ), 0)
    query = lax.broadcasted_iota(jnp.int32, (SEQ, SEQ), 1)
    allowed = key <= query
    units = units_of(step, n_seqs)

    def scores(rows, pair):
        c = pair * LN
        return dot_last(qkv[rows, D + c:D + c + LN], block_diag(qkv[rows, c:c + LN]))

    ahead = 2
    pending = [scores(*u) for u in units[:ahead]]
    for i, (rows, pair) in enumerate(units):
        if i + ahead < len(units):
            pending.append(scores(*units[i + ahead]))
        s = pending[i]
        c = pair * LN
        probs = []
        for head in range(2):
            sh = jnp.where(allowed, s[:, head * LN:head * LN + LN], -1e30)
            e = jnp.exp2((sh - jnp.max(sh, axis=0, keepdims=True)) * EXP2_SCALE)
            p = e * (1.0 / jnp.sum(e, axis=0, keepdims=True))
            p_out[rows, 2 * c + head * LN:2 * c + head * LN + LN] = p
            probs.append(p.astype(BF16))
        v = qkv[rows, 2 * D + c:2 * D + c + LN]
        o_out[rows, c:c + LN] = dot_first(jnp.concatenate(probs, axis=0), block_diag(v)).astype(BF16)


def attention_bwd(step, n_seqs, qkv, p_in, do):
    units = units_of(step, n_seqs)

    def first(rows, pair):
        c = pair * LN
        d = block_diag(do[rows, c:c + LN])
        return d, dot_last(qkv[rows, 2 * D + c:2 * D + c + LN], d)

    ahead = 2
    pending = [first(*u) for u in units[:ahead]]
    for i, (rows, pair) in enumerate(units):
        if i + ahead < len(units):
            pending.append(first(*units[i + ahead]))
        d, dp = pending[i]
        c = pair * LN
        q = qkv[rows, c:c + LN]
        k = qkv[rows, D + c:D + c + LN]
        p = p_in[rows, 2 * c:2 * c + 256]
        dv = dot(p.astype(BF16), d).astype(BF16)
        pd = p * dp
        ds = ((pd - p * jnp.sum(pd, axis=0, keepdims=True)) * HD ** -0.5).astype(BF16)
        dk = dot(ds, block_diag(q)).astype(BF16)
        dq = dot_first(jnp.concatenate([ds[:, :LN], ds[:, LN:]], axis=0), block_diag(k)).astype(BF16)
        qkv[rows, c:c + LN] = dq
        qkv[rows, D + c:D + c + LN] = dk
        qkv[rows, 2 * D + c:2 * D + c + LN] = dv


AXES = (("x", "y", "z"), ("y", "z", "x"), ("z", "x", "y"))
NAT = ("z", "y", "x")
STRIDE = {"x": 1, "y": 4, "z": 16}
UNITS = [(colour, way) for colour in range(3) for way in (1, -1)]


class Place:
    def __init__(self):
        self.core = lax.axis_index("pp")
        self.dp = lax.axis_index("dp")
        self.at = {"x": lax.rem(self.dp, 4), "y": lax.rem(self.dp // 4, 4), "z": self.dp // 16}

    def neighbour(self, axis, way):
        c = self.at[axis]
        return (self.core, self.dp + (lax.rem(c + way + 4, 4) - c) * STRIDE[axis])

    def partner(self):
        return (1 - self.core, self.dp)

    def block(self, axis, way, step):
        return lax.rem(self.at[axis] - way * (1 + step) + 8, 4)


def greet(peers):
    barrier = pltpu.get_barrier_semaphore()
    for p in peers:
        pl.semaphore_signal(barrier, inc=1, device_id=p, device_id_type=MESH)
    pl.semaphore_wait(barrier, len(peers))


CHUNKS = 16
STREAMS = 4
POS = {0: 0, 3: 1, 2: 2, 1: 3}
J0 = {0: 0, 3: 0, 2: 1, 1: 2}


HOP = (16, 4, 1)
FROM = (0, 16, 20)
LINK = 21


def ring_scratch():
    return [
        pltpu.VMEM((STREAMS, NU, LINK) + TILE, F32), pltpu.VMEM((STREAMS, 2, NU, LINK) + TILE, F32),
        pltpu.VMEM((STREAMS, NU, 4, 4) + TILE, F32), pltpu.VMEM((STREAMS, NU, 4) + TILE, F32),
        pltpu.SemaphoreType.DMA((STREAMS,)), pltpu.SemaphoreType.DMA((STREAMS, 2)),
    ]


def pick_block(ref, axis, b):
    return {"z": lambda: ref[b], "y": lambda: ref[:, b], "x": lambda: ref[:, :, b]}[axis]()


class Rings:
    def __init__(self, place, scratch, own, ready, done):
        self.p, self.own, self.ready, self.done = place, own, ready, done
        self.sent, self.got, self.t1, self.t2, self.ss, self.rs = scratch
        self.sent[:, :, FROM[1]:] = jnp.zeros((STREAMS, NU, LINK - FROM[1]) + TILE, F32)

    def links(self, e, par, link, lo):
        tiles = pl.ds(lo, LINK - lo)
        axis, way = UNITS[0 if link is None else link]
        at = slice(None) if link is None else link
        return pltpu.make_async_remote_copy(self.sent.at[e, at, tiles], self.got.at[e, par, at, tiles], self.ss.at[e], self.rs.at[e, par],
                                            device_id=self.p.neighbour("xyz"[axis], way), device_id_type=MESH)

    def wait(self, e, par, lo):
        c = self.links(e, par, None, lo)
        c.wait_send()
        c.wait_recv()

    def send(self, e, par, lo):
        for link in range(NU):
            self.links(e, par, link, lo).start()

    def link(self, u, phase):
        return (u + 2 * phase) % NU

    def came(self, e, par, u, phase):
        lo = FROM[phase]
        v = self.got[e, par, self.link(u, phase), lo:lo + HOP[phase]]
        return v.reshape(((4, 4), (4,), ())[phase] + TILE)

    def go(self, e, u, phase, value):
        lo = FROM[phase]
        self.sent[e, self.link(u, phase), lo:lo + HOP[phase]] = value.reshape((HOP[phase],) + TILE)

    def block(self, u, phase, step):
        colour, way = UNITS[u]
        return self.p.block(AXES[colour][phase], way, step)

    def first(self, own, u, step):
        return pick_block(own.at[u], AXES[UNITS[u][0]][0], self.block(u, 0, step))

    def second(self, e, u, step):
        order = AXES[UNITS[u][0]]
        b = self.block(u, 1, step)
        rest = [a for a in NAT if a != order[0]]
        return self.t1[e, u, :, b] if rest.index(order[1]) == 1 else self.t1[e, u, b]

    def third(self, e, u, step):
        return self.t2[e, u, self.block(u, 2, step)]

    def slot(self, n, iteration):
        e, j = n % STREAMS, n // STREAMS
        step = (j - J0[e]) % 3
        k = iteration + (j - J0[e]) // 3
        par = lax.rem(3 * iteration + j, 2)
        old = 1 - par
        chunk = lambda i: STREAMS * (k - i) + POS[e]
        live = lambda i: (chunk(i) >= 0) & (chunk(i) < CHUNKS)
        new = 1 if step == 0 else 0

        @pl.when(live(new))
        def _():
            self.wait(e, old, 0)

        @pl.when(jnp.logical_not(live(new)) & (live(new + 1) | live(new + 2)))
        def _():
            self.wait(e, old, FROM[1])

        if step == 0:
            @pl.when(live(3))
            def _():
                for u in range(NU):
                    self.done[chunk(3), u] = self.came(e, old, u, 2) + self.third(e, u, 3)

            @pl.when(live(2))
            def _():
                for u in range(NU):
                    self.t2[e, u] = self.came(e, old, u, 1) + self.second(e, u, 3)
                    self.go(e, u, 2, self.third(e, u, 0))

            @pl.when(live(1))
            def _():
                own = self.own(chunk(1))
                for u in range(NU):
                    self.t1[e, u] = self.came(e, old, u, 0) + self.first(own, u, 3)
                    self.go(e, u, 1, self.second(e, u, 0))

            @pl.when(live(0))
            def _():
                self.ready(chunk(0))
                own = self.own(chunk(0))
                for u in range(NU):
                    self.go(e, u, 0, self.first(own, u, 0))
        else:
            @pl.when(live(2))
            def _():
                for u in range(NU):
                    self.go(e, u, 2, self.came(e, old, u, 2) + self.third(e, u, step))

            @pl.when(live(1))
            def _():
                for u in range(NU):
                    self.go(e, u, 1, self.came(e, old, u, 1) + self.second(e, u, step))

            @pl.when(live(0))
            def _():
                own = self.own(chunk(0))
                for u in range(NU):
                    self.go(e, u, 0, self.came(e, old, u, 0) + self.first(own, u, step))

        @pl.when(live(0))
        def _():
            self.send(e, par, 0)

        @pl.when(jnp.logical_not(live(0)) & (live(1) | live(2)))
        def _():
            self.send(e, par, FROM[1])


def tiles_of_layer():
    down = [(3, g, j) for j in range(4) for g in range(4)]
    up = [(2, 0, j) for j in range(16)]
    out = [(1, 0, j) for j in range(4)]
    qkv = [(0, 0, j) for j in range(12)]
    return down + up + out + qkv


TILES = tiles_of_layer()
PLACE_OF = {t: (i // 12, i % 12 // 6, i % 6) for i, t in enumerate(TILES)}


FWD_SEQS = 3
BWD_SEQS = 2
OWN_SLOTS = 8
DRAIN = 3
QKV_W, OUT_W, UP_W, DOWN_W = range(4)
HALF = 2 * D


def step_kernel(x, seed, wq, wo, wu, wd,
                y, rq, ro, ru, rd, hs, qs, ps, os, ms, us, out,
                grads, recv, done, h, qkv, p, o, m, u, e, g, g1, do, acc, vq, vo, vu, vd,
                wsem, asem, gsem, psem, qsem, hsem, ysem, dsend, drecv, fsem, credit, *ring):
    place = Place()
    core = place.core
    partner = place.partner()
    mine = (wq, wo, wu, wd)
    theirs = (rq, ro, ru, rd)
    held = (vq, vo, vu, vd)
    acts = ((h, hs), (qkv, qs), (p, ps), (o, os), (m, ms), (u, us))
    H, QKV, PROB, O, M, U = range(6)
    rows = pl.ds(core * ROWS, ROWS)

    def to_partner(src, dst, send, arrive):
        return pltpu.make_async_remote_copy(src, dst, send, arrive, device_id=partner, device_id_type=MESH)

    def push(k, j):
        return to_partner(mine[k].at[j], theirs[k].at[j], psem.at[k, j], qsem.at[k, j])

    halves = [(UP_W, (slice(None), pl.ds(0, HALF))), (DOWN_W, (pl.ds(0, HALF),)),
              (UP_W, (slice(None), pl.ds(HALF, HALF))), (DOWN_W, (pl.ds(HALF, HALF),))]
    direct = [(QKV_W, ()), (OUT_W, ())] + halves

    def hand(i):
        k, at = direct[i]
        src, dst = mine[k].at[0], held[k]
        if at:
            src, dst = src.at[at], dst.at[at]
        return to_partner(src, dst, hsem.at[0, i], hsem.at[1, i])

    def local_w(k, l, src):
        return pltpu.make_async_copy(src[k].at[lax.rem(l, 2)], held[k], wsem.at[k])

    def fetch_w(k, l, arrives):
        @pl.when(l // 2 == core)
        def _():
            local_w(k, l, mine).start()

        @pl.when(l // 2 != core)
        def _():
            @pl.when(arrives)
            def _():
                push(k, lax.rem(l, 2)).wait_recv()
            local_w(k, l, theirs).start()

    def wait_w(k):
        local_w(k, 0, mine).wait()

    def act(i, l, back):
        vmem, hbm = acts[i]
        return pltpu.make_async_copy(hbm.at[l], vmem, asem.at[i]) if back else pltpu.make_async_copy(vmem, hbm.at[l], asem.at[i])

    def own_slot(chunk):
        return lax.rem(chunk, OWN_SLOTS)

    def cross(chunk):
        q = lax.rem(chunk, 4)
        return to_partner(grads.at[OWN_SLOTS + q], recv.at[q], dsend.at[q], drecv.at[q])

    def ready(chunk):
        q = lax.rem(chunk, 4)
        cross(chunk).wait_recv()
        for unit in range(NU):
            grads[own_slot(chunk), unit] = grads[own_slot(chunk), unit] + recv[q, unit]

        @pl.when(chunk + 4 < CHUNKS)
        def _():
            pl.semaphore_signal(credit.at[q], inc=1, device_id=partner, device_id_type=MESH)

    rings = Rings(place, ring, lambda chunk: grads.at[own_slot(chunk)], ready, done)

    x_in = pltpu.make_async_copy(x.at[rows], h, asem.at[H])
    x_in.start()
    seed_in = pltpu.make_async_copy(seed.at[rows], g, gsem)

    @pl.when(core == 0)
    def _():
        for k in range(4):
            local_w(k, 0, mine).start()
    greet([partner] + [place.neighbour(a, way) for a in NAT for way in (1, -1)])

    @pl.when(core == 0)
    def _():
        for i in range(len(direct)):
            hand(i).start()
        for j in (1, 0):
            for k in range(4):
                push(k, j).start()

    @pl.when(core == 1)
    def _():
        for j in range(2):
            for k in range(4):
                push(k, j).start()
    seed_in.start()
    x_in.wait()

    def layer(l, _):
        handed = (l == 0) & (core == 1)

        def weight(k, parts=()):
            @pl.when(jnp.logical_not(handed))
            def _():
                wait_w(k)

            @pl.when(handed)
            def _():
                for i in parts or (k,):
                    hand(i).wait_recv()

        def again(i):
            @pl.when(l > 0)
            def _():
                act(i, l - 1, False).wait()

        def save(i):
            @pl.when(l < LAYERS - 1)
            def _():
                act(i, l, False).start()

        def next_w(*ks):
            @pl.when(l < LAYERS - 1)
            def _():
                for k in ks:
                    fetch_w(k, l + 1, True)

        again(H)

        @pl.when(l > 0)
        def _():
            h[...] = do[...]
        save(H)
        weight(QKV_W)
        again(QKV)
        hf = h[...].astype(F32)
        qkv[...] = dot((hf * inv_rms(hf)).astype(BF16), vq[...]).astype(BF16)
        save(QKV)
        again(PROB)
        again(O)

        def attend(i, _):
            attention_fwd(i, FWD_SEQS, qkv, p, o)
            return 0

        lax.fori_loop(0, NSEQ // FWD_SEQS, attend, 0)
        save(PROB)
        save(O)
        weight(OUT_W)
        again(M)
        m[...] = (h[...].astype(F32) + dot(o[...], vo[...])).astype(BF16)
        save(M)
        again(U)
        weight(UP_W, (2, 3))

        @pl.when(jnp.logical_not(handed))
        def _():
            wait_w(DOWN_W)

        def mlp(j):
            cols = slice(j * HALF, (j + 1) * HALF)
            mf = m[...].astype(F32)
            c = (mf * inv_rms(mf)).astype(BF16)
            ub = dot(c, vu[:, cols]).astype(BF16)
            u[:, cols] = ub
            eb = gelu(ub.astype(F32)).astype(BF16)
            e[:, cols] = eb
            return dot(eb, vd[cols, :])

        acc[...] = m[...].astype(F32) + mlp(0)
        next_w(QKV_W, OUT_W)

        @pl.when(handed)
        def _():
            hand(4).wait_recv()
            hand(5).wait_recv()
        do[...] = (acc[...] + mlp(1)).astype(BF16)
        save(U)
        next_w(UP_W, DOWN_W)
        return 0

    lax.fori_loop(0, LAYERS, layer, 0)
    y_here = pltpu.make_async_copy(do, y.at[rows], ysem.at[0])
    y_there = to_partner(do, y.at[rows], ysem.at[1], ysem.at[2])
    y_here.start()
    y_there.start()

    def free(chunk):
        @pl.when(chunk >= 4)
        def _():
            cross(chunk).wait_send()

    def put(base, tile, value):
        q, half, unit = PLACE_OF[tile]
        index = jnp.where(core == half, own_slot(base + q), OWN_SLOTS + q)
        grads[index, unit] = value.reshape((4, 4, 4) + TILE)

    def ship(chunk):
        @pl.when(chunk >= 4)
        def _():
            pl.semaphore_wait(credit.at[lax.rem(chunk, 4)], 1)
        cross(chunk).start()

    def down_grad(base):
        free(base)
        free(base + 1)
        for half in range(2):
            w = dot_first(e[...], g[:, half * 256:half * 256 + 256]).reshape((64, 4, 8, 256))
            for j in range(2):
                for rg in range(4):
                    put(base, (DOWN_W, rg, 2 * half + j), w[:, rg, :, j * LN:j * LN + LN])
        ship(base)

    def gelu_part(j):
        cols = slice(j * D, (j + 1) * D)
        de = dot_last(g[...], vd[cols, :])
        ej, slope = gelu_and_slope(u[:, cols].astype(F32))
        e[:, cols] = ej.astype(BF16)
        u[:, cols] = (slope * de).astype(BF16)

    def wide_grad(base, array, a, b, parts):
        for part in range(parts):
            w = dot_first(a, b[:, part * D:part * D + D]).reshape((64, 8, D))
            for j in range(4):
                put(base, (array, 0, 4 * part + j), w[:, :, j * LN:j * LN + LN])

    seed_in.wait()
    down_grad(0)
    for j in range(4):
        gelu_part(j)
    y_here.wait()
    y_there.wait_send()

    def iteration(it, _):
        l = LAYERS - 1 - it
        more = it < LAYERS - 1
        base = 4 * it

        def loaded(acts_of, w=None):
            @pl.when(it > 0)
            def _():
                for i in acts_of:
                    act(i, l, True).wait()
                if w is not None:
                    wait_w(w)

        def after(acts_of, *ws):
            @pl.when(more)
            def _():
                for k in ws:
                    fetch_w(k, l - 1, l == 1)
                for i in acts_of:
                    act(i, l - 1, True).start()

        def piece(n):
            if n == 0:
                loaded((M,))
                free(base + 2)
                mf = m[...].astype(F32)
                wide_grad(base, UP_W, (mf * inv_rms(mf)).astype(BF16), u, 4)
                ship(base + 1)
            elif n == 1:
                loaded((), UP_W)
                dc = dot_last(u[...], vu[...])
                g1[...] = (g[...].astype(F32) + rms_bwd(m[...].astype(F32), dc)).astype(BF16)
                after((U, M), UP_W, DOWN_W)
            elif n == 2:
                loaded((O,), OUT_W)
                do[...] = dot_last(g1[...], vo[...]).astype(BF16)
                wide_grad(base, OUT_W, o[...], g1, 1)
                ship(base + 2)
                after((O,), OUT_W)
            elif n in (3, 4, 5):
                if n == 3:
                    loaded((PROB, QKV))
                attention_bwd(n - 3, BWD_SEQS, qkv, p, do)
                if n == 5:
                    after((PROB,))
            elif n == 6:
                loaded((H,), QKV_W)
                da = dot_last(qkv[...], vq[...])
                g[...] = (g1[...].astype(F32) + rms_bwd(h[...].astype(F32), da)).astype(BF16)
                after((), QKV_W)
            elif n == 7:
                free(base + 3)
                hf = h[...].astype(F32)
                wide_grad(base, QKV_W, (hf * inv_rms(hf)).astype(BF16), qkv, 3)
                ship(base + 3)
                after((H, QKV))
            elif n in (8, 9):
                @pl.when(more)
                def _():
                    if n == 8:
                        act(U, l - 1, True).wait()
                        wait_w(DOWN_W)
                    for j in range(2):
                        gelu_part(2 * (n - 8) + j)
            elif n == 10:
                @pl.when(more)
                def _():
                    down_grad(base + 4)

        for n in range(12):
            rings.slot(n, it)
            if n < 11:
                @pl.when(it < LAYERS)
                def _():
                    piece(n)
        return 0

    lax.fori_loop(0, LAYERS + DRAIN, iteration, 0)

    for q in range(4):
        cross(CHUNKS - 4 + q).wait_send()
    last = to_partner(done.at[pl.ds(8 * core, 8)], out.at[core], fsem.at[0], fsem.at[1])
    last.start()
    out[core] = done[pl.ds(8 * (1 - core), 8)]
    for j in range(2):
        for k in range(4):
            push(k, j).wait_send()

    @pl.when(core == 0)
    def _():
        for i in range(len(direct)):
            hand(i).wait_send()
    y_there.wait_recv()
    last.wait_send()
    last.wait_recv()


def train_step(x, seed, weights):
    anywhere = pl.BlockSpec(memory_space=pl.ANY)
    vmem = pl.BlockSpec(memory_space=pltpu.VMEM)
    act = lambda cols, dt=BF16: pltpu.VMEM((ROWS, cols), dt)
    saved = lambda cols, dt=BF16: jax.ShapeDtypeStruct((LAYERS - 1, ROWS, cols), dt)
    outs = pl.pallas_call(
        step_kernel,
        name="step",
        out_shape=[jax.ShapeDtypeStruct((2 * ROWS, D), BF16)] + [jax.ShapeDtypeStruct((2,) + s, BF16) for s in W_SHAPES]
        + [saved(D), saved(3 * D), saved(2 * D, F32), saved(D), saved(D), saved(4 * D)]
        + [jax.ShapeDtypeStruct((2, 8, NU) + TILE, F32)],
        in_specs=[anywhere] * 6,
        out_specs=[anywhere] * 11 + [vmem],
        scratch_shapes=[
            pltpu.VMEM((OWN_SLOTS + 4, NU, 4, 4, 4) + TILE, F32),
            pltpu.VMEM((4, NU, 4, 4, 4) + TILE, F32),
            pltpu.VMEM((CHUNKS, NU) + TILE, F32),
            act(D), act(3 * D), act(2 * D, F32), act(D), act(D), act(4 * D), act(4 * D), act(D), act(D), act(D), act(D, F32),
        ] + [pltpu.VMEM(s, BF16) for s in W_SHAPES] + [
            pltpu.SemaphoreType.DMA((4,)), pltpu.SemaphoreType.DMA((6,)), pltpu.SemaphoreType.DMA,
            pltpu.SemaphoreType.DMA((4, 2)), pltpu.SemaphoreType.DMA((4, 2)), pltpu.SemaphoreType.DMA((2, 6)),
            pltpu.SemaphoreType.DMA((3,)),
            pltpu.SemaphoreType.DMA((4,)), pltpu.SemaphoreType.DMA((4,)), pltpu.SemaphoreType.DMA((2,)),
            pltpu.SemaphoreType.REGULAR((4,)),
        ] + ring_scratch(),
        compiler_params=pltpu.CompilerParams(collective_id=1, has_side_effects=True, vmem_limit_bytes=67043328),
    )(x, seed, *weights)
    return outs[0], outs[-1]


def finish_kernel(y_in, sums, y, gq, go, gu, gd, buf, in_sem, out_sem):
    parts = buf.shape[0]
    move = lambda i, into: (pltpu.make_async_copy(y_in.at[i], buf.at[i], in_sem.at[i]) if into
                            else pltpu.make_async_copy(buf.at[i], y.at[i], out_sem.at[i]))
    for i in range(parts):
        move(i, True).start()
    outs = (gq, go, gu, gd)
    for layer in range(2):
        for tile in TILES:
            array, rg, col = tile
            q, half, unit = PLACE_OF[tile]
            outs[array][layer, rg * 8:rg * 8 + 8, col * LN:col * LN + LN] = sums[half, 4 * (1 - layer) + q, unit]
    for i in range(parts):
        move(i, True).wait()
        move(i, False).start()
    for i in range(parts):
        move(i, False).wait()


def finish(y, sums, parts=4):
    anywhere = pl.BlockSpec(memory_space=pl.ANY)
    vmem = pl.BlockSpec(memory_space=pltpu.VMEM)
    shape = (parts, 2 * ROWS // parts, D)
    return pl.pallas_call(
        finish_kernel,
        name="finish",
        out_shape=[jax.ShapeDtypeStruct(shape, BF16)]
        + [jax.ShapeDtypeStruct(s, F32) for s in ((2, 8, 3 * D), (2, 8, D), (2, 8, 4 * D), (2, 32, D))],
        in_specs=[anywhere, vmem],
        out_specs=[anywhere] + [vmem] * 4,
        scratch_shapes=[pltpu.VMEM(shape, BF16), pltpu.SemaphoreType.DMA((parts,)), pltpu.SemaphoreType.DMA((parts,))],
    )(y.reshape(shape), sums)


def solution(mesh):
    def step(x_in, seed_grad, w_qkv, w_out, w_up, w_down):
        shape = x_in.shape
        weights = (w_qkv, w_out, w_up, w_down)
        y, sums = train_step(x_in.reshape(2 * ROWS, D), seed_grad.reshape(2 * ROWS, D), weights)
        y, *grads = finish(y, sums)
        return y.reshape(shape), *grads

    act, weight, grad = P(None, "dp"), P("pp"), P("pp", "dp")
    return jax.shard_map(
        step,
        mesh=mesh,
        in_specs=(act, act, weight, weight, weight, weight),
        out_specs=(act, grad, grad, grad, grad),
        check_vma=False,
    )
```

time: 201 us -> 192 us (0.955)
  local copies, waits for them, and re-layouts: 5.29 us -> 0 us
  Pallas kernels: 195 us -> 191 us
    unnamed x13 -> x0, local copies, waits for them, and re-layouts: 5.29 us -> none
    pallas_call x2, Pallas kernels: 195 us -> 191 us  [the longest x1 187 us: train_step(): pl.pallas_call(step_kernel, name='step', out_shape=[jax.ShapeDtypeStruct(...]
where the time goes in v2:
time: 192 us
  Pallas kernels  191 us (99%)
    pallas_call x1, Pallas kernels, train_step(): pl.pallas_call(step_kernel, name='step', out_shape=[jax.ShapeDtypeStruct(...  187 us
    pallas_call x1, Pallas kernels, finish(): pl.pallas_call(finish_kernel, name='finish', out_shape=[jax.ShapeDtypeStr...  3.94 us

profile of v2, /device:TPU:1, one launch (start us, length us, event | category | flops | bytes accessed | tf_op | source)
XLA Modules:
  0.0 191.5 jit_solution(1603092481363496385)
XLA Ops:
  0.6 186.8 %step.1 = (bf16[1536,512]{1,0:T(8,128)(2,1)}, bf16[2,512,1536]{2,1,0:T(8,128)(2,1)}, bf16[2,512,512]{2,1,0:T(8,128)(2,1)}, bf16[2,512,2048]{2,1,0:T(8,128)(2,1)}...) custom-call(bf16[1536,512]{1,0:T(8,128)(2,1)} %bitcast.7, ...), custom_call_target="tpu_custom_call" | custom-call | tf_op jit(solution)/shard_map/step/pallas_call | solution.py:661
  187.4 3.9 %finish.1 = (bf16[4,384,512]{2,1,0:T(8,128)(2,1)}, f32[2,8,1536]{2,1,0:T(8,128)}, f32[2,8,512]{2,1,0:T(8,128)}, f32[2,8,2048]{2,1,0:T(8,128)}, f32[2,32,512]{2,1,0:T(8,128)}) custom-call(bf16[4,384,512]{2,1,0:T(8,128)(2,1)} %bitcast.6, f32[2,8,6,8,128]{4,3,2,1,0:T(8,128)} %get-tuple-element.13.sums), custom_call_target="tpu_custom_call" | custom-call | tf_op jit(solution)/shard_map/finish/pallas_call | solution.py:709

commit v3 on v2

v3 whole, which is shorter than its diff:
```python
import functools
import math

import jax
import jax.numpy as jnp
from jax import lax
from jax.experimental import pallas as pl
from jax.experimental.pallas import tpu as pltpu
from jax.sharding import PartitionSpec as P

F32 = jnp.float32
BF16 = jnp.bfloat16
MESH = pl.DeviceIdType.MESH

D = 512
HD = 64
LN = 128
TILE = (8, LN)
QUAD = 4
PLANE = (QUAD, QUAD)
CUBE = PLANE + (QUAD,)
NU = 6
SEQ = LN
NSEQ = 6
ROWS = NSEQ * SEQ
LAYERS = 4
EPS = 1e-6
GELU_C1 = math.sqrt(2.0 / math.pi)
GELU_C2 = GELU_C1 * 0.044715
EXP2_SCALE = HD ** -0.5 * math.log2(math.e)
W_SHAPES = ((D, 3 * D), (D, D), (D, QUAD * D), (QUAD * D, D))
LAST = (((1,), (1,)), ((), ()))
FIRST = (((0,), (0,)), ((), ()))


def dot(a, b):
    return jnp.dot(a, b, preferred_element_type=F32)


def dot_last(a, b):
    return lax.dot_general(a, b, LAST, preferred_element_type=F32)


def dot_first(a, b):
    return lax.dot_general(a, b, FIRST, preferred_element_type=F32)


def inv_rms(h):
    return lax.rsqrt(jnp.mean(h * h, axis=-1, keepdims=True) + EPS)


def rms_bwd(h, g):
    ir = inv_rms(h)
    n = h * ir
    return ir * (g - n * jnp.mean(g * n, axis=-1, keepdims=True))


def gelu(u):
    t = jnp.tanh(u * (GELU_C1 + GELU_C2 * (u * u)))
    return u * (0.5 * t + 0.5)


def gelu_slope(u):
    a = GELU_C2 * (u * u)
    t = jnp.tanh(u * (a + GELU_C1))
    half = 0.5 * t + 0.5
    return half + u * half * (1.0 - t) * (3.0 * a + GELU_C1)


def block_diag(x):
    first = lax.broadcasted_iota(jnp.int32, (SEQ, 2 * HD), 1) < HD
    zero = jnp.zeros_like(x)
    return jnp.concatenate([jnp.where(first, x, zero), jnp.where(first, zero, x)], axis=0)


def units_of(step, n_seqs):
    return [(pl.ds(pl.multiple_of((step * n_seqs + n) * SEQ, SEQ), SEQ), pair) for n in range(n_seqs) for pair in range(QUAD)]


def attention_fwd(step, n_seqs, qkv, p_out, o_out):
    key = lax.broadcasted_iota(jnp.int32, (SEQ, SEQ), 0)
    query = lax.broadcasted_iota(jnp.int32, (SEQ, SEQ), 1)
    allowed = key <= query
    units = units_of(step, n_seqs)

    def scores(rows, pair):
        c = pair * LN
        return dot_last(qkv[rows, D + c:D + c + LN], block_diag(qkv[rows, c:c + LN]))

    ahead = 2
    pending = [scores(*u) for u in units[:ahead]]
    for i, (rows, pair) in enumerate(units):
        if i + ahead < len(units):
            pending.append(scores(*units[i + ahead]))
        s = pending[i]
        c = pair * LN
        probs = []
        for head in range(2):
            sh = jnp.where(allowed, s[:, head * LN:head * LN + LN], -1e30)
            e = jnp.exp2((sh - jnp.max(sh, axis=0, keepdims=True)) * EXP2_SCALE)
            p = e * (1.0 / jnp.sum(e, axis=0, keepdims=True))
            p_out[rows, 2 * c + head * LN:2 * c + head * LN + LN] = p
            probs.append(p.astype(BF16))
        v = qkv[rows, 2 * D + c:2 * D + c + LN]
        o_out[rows, c:c + LN] = dot_first(jnp.concatenate(probs, axis=0), block_diag(v)).astype(BF16)


def attention_bwd(step, n_seqs, qkv, p_in, do):
    units = units_of(step, n_seqs)

    def first(rows, pair):
        c = pair * LN
        d = block_diag(do[rows, c:c + LN])
        return d, dot_last(qkv[rows, 2 * D + c:2 * D + c + LN], d)

    ahead = 2
    pending = [first(*u) for u in units[:ahead]]
    for i, (rows, pair) in enumerate(units):
        if i + ahead < len(units):
            pending.append(first(*units[i + ahead]))
        d, dp = pending[i]
        c = pair * LN
        q = qkv[rows, c:c + LN]
        k = qkv[rows, D + c:D + c + LN]
        p = p_in[rows, 2 * c:2 * c + 256]
        dv = dot(p.astype(BF16), d).astype(BF16)
        pd = p * dp
        ds = ((pd - p * jnp.sum(pd, axis=0, keepdims=True)) * HD ** -0.5).astype(BF16)
        dk = dot(ds, block_diag(q)).astype(BF16)
        dq = dot_first(jnp.concatenate([ds[:, :LN], ds[:, LN:]], axis=0), block_diag(k)).astype(BF16)
        qkv[rows, c:c + LN] = dq
        qkv[rows, D + c:D + c + LN] = dk
        qkv[rows, 2 * D + c:2 * D + c + LN] = dv


AXES = (("x", "y", "z"), ("y", "z", "x"), ("z", "x", "y"))
NAT = ("z", "y", "x")
STRIDE = {"x": 1, "y": 4, "z": 16}
UNITS = [(colour, way) for colour in range(3) for way in (1, -1)]


class Place:
    def __init__(self):
        self.core = lax.axis_index("pp")
        self.dp = lax.axis_index("dp")
        self.at = {"x": lax.rem(self.dp, QUAD), "y": lax.rem(self.dp // QUAD, QUAD), "z": self.dp // 16}

    def neighbour(self, axis, way):
        c = self.at[axis]
        return (self.core, self.dp + (lax.rem(c + way + QUAD, QUAD) - c) * STRIDE[axis])

    def partner(self):
        return (1 - self.core, self.dp)

    def block(self, axis, way, step):
        return lax.rem(self.at[axis] - way * (1 + step) + 8, QUAD)


def greet(peers):
    barrier = pltpu.get_barrier_semaphore()
    for p in peers:
        pl.semaphore_signal(barrier, inc=1, device_id=p, device_id_type=MESH)
    pl.semaphore_wait(barrier, len(peers))


CHUNKS = 16
PERIOD = 3
STREAMS = 4
SLOTS = PERIOD * CHUNKS
HOP = (16, 4, 1)
FROM = (0, 16, 20)
LINK = 21


def ring_scratch():
    dma = pltpu.SemaphoreType.DMA
    return [
        pltpu.VMEM((STREAMS, NU, LINK) + TILE, F32), pltpu.VMEM((STREAMS, 2, NU, LINK) + TILE, F32),
        pltpu.VMEM((STREAMS, NU) + PLANE + TILE, F32), pltpu.VMEM((STREAMS, NU, 4) + TILE, F32),
        pltpu.VMEM((STREAMS, 3, NU, 4) + TILE, F32), pltpu.VMEM((2, STREAMS, 3, NU) + TILE, F32),
        dma((STREAMS,)), dma((STREAMS, 2)), dma((3, STREAMS)), dma((3, STREAMS)),
    ]


def pick_block(ref, axis, b):
    return {"z": lambda: ref[b], "y": lambda: ref[:, b], "x": lambda: ref[:, :, b]}[axis]()


class Rings:
    def __init__(self, place, scratch, own, ready, done):
        self.p, self.own, self.ready, self.done = place, own, ready, done
        self.sent, self.got, self.t1, self.t2, self.d2, self.d3, self.ss, self.rs, self.ds, self.dr = scratch
        self.sent[:, :, FROM[1]:] = jnp.zeros((STREAMS, NU, LINK - FROM[1]) + TILE, F32)

    def links(self, e, par, link, lo):
        tiles = pl.ds(lo, LINK - lo)
        axis, way = UNITS[0 if link is None else link]
        at = slice(None) if link is None else link
        return pltpu.make_async_remote_copy(self.sent.at[e, at, tiles], self.got.at[e, par, at, tiles], self.ss.at[e], self.rs.at[e, par],
                                            device_id=self.p.neighbour("xyz"[axis], way), device_id_type=MESH)

    def wait(self, e, par, lo):
        c = self.links(e, par, None, lo)
        c.wait_send()
        c.wait_recv()

    def send(self, e, par, lo):
        for link in range(NU):
            self.links(e, par, link, lo).start()

    def link(self, u, phase):
        return (u + 2 * phase) % NU

    def came(self, e, par, u, phase):
        lo = FROM[phase]
        v = self.got[e, par, self.link(u, phase), lo:lo + HOP[phase]]
        return v.reshape((PLANE, PLANE[1:], ())[phase] + TILE)

    def go(self, e, u, phase, value):
        lo = FROM[phase]
        self.sent[e, self.link(u, phase), lo:lo + HOP[phase]] = value.reshape((HOP[phase],) + TILE)

    def block(self, u, phase, step):
        colour, way = UNITS[u]
        return self.p.block(AXES[colour][phase], way, step)

    def first(self, own, u, step):
        return pick_block(own.at[u], AXES[UNITS[u][0]][0], self.block(u, 0, step))

    def second_ref(self, e, u, b):
        order = AXES[UNITS[u][0]]
        rest = [a for a in NAT if a != order[0]]
        return self.t1.at[(e, u, slice(None), b) if rest.index(order[1]) == 1 else (e, u, b)]

    def second(self, e, u, step):
        return self.second_ref(e, u, self.block(u, 1, step))[...]

    def third(self, e, u, step):
        return self.t2[e, u, self.block(u, 2, step)]

    def straight(self, e, kind, u, j):
        phase = 1 if kind == 0 else 2
        axis = AXES[UNITS[u][0]][phase]
        b = lax.rem(self.p.at[axis] + j, QUAD)
        src = self.second_ref(e, u, b) if kind == 0 else self.t2.at[e, u, b]
        dst = self.landing(e, kind).at[j - 1, u]
        return pltpu.make_async_remote_copy(src, dst, self.ds.at[kind, e], self.dr.at[kind, e],
                                            device_id=self.p.neighbour(axis, j), device_id_type=MESH)

    def landing(self, e, kind):
        return self.d2.at[e] if kind == 0 else self.d3.at[kind - 1, e]

    def go_straight(self, e, kind):
        for j in (1, 3, 2):
            for u in range(NU):
                self.straight(e, kind, u, j).start()

    def wait_straight(self, e, kind):
        at = self.landing(e, kind)
        c = pltpu.make_async_remote_copy(at, at, self.ds.at[kind, e], self.dr.at[kind, e],
                                         device_id=self.p.neighbour("x", 1), device_id_type=MESH)
        c.wait_send()
        c.wait_recv()

    def sum_straight(self, e, kind, u):
        at = self.landing(e, kind)
        return at[0, u] + at[1, u] + at[2, u]

    def slot(self, s, step, drain=False):
        e = lax.rem(s, STREAMS)
        par = lax.rem(s // STREAMS, 2)
        old = 1 - par
        since = s - STREAMS * step
        chunk = lambda i: since // PERIOD - STREAMS * i
        live = lambda i: (since >= PERIOD * STREAMS * i) & (chunk(i) < CHUNKS)
        early = lambda i: chunk(i) < CHUNKS - 2 * STREAMS
        not_late = lambda i: chunk(i) < CHUNKS - STREAMS
        if not drain:
            early = not_late = lambda i: True
        both = lambda a, b: a if b is True else a & b
        ring1 = both(live(1), not_late(1))
        ring2 = both(live(2), early(2))
        late = live(1) & jnp.logical_not(not_late(1)) if drain else None
        middle = live(2) & not_late(2) & jnp.logical_not(early(2)) if drain else None
        if step == 0:
            was, more = live(1), both(live(2), not_late(2)) | both(live(3), early(3))
        else:
            was, more = live(0), ring1 | ring2

        @pl.when(was)
        def _():
            self.wait(e, old, 0)

        @pl.when(jnp.logical_not(was) & more)
        def _():
            self.wait(e, old, FROM[1])

        if step == 0:
            @pl.when(both(live(3), early(3)))
            def _():
                for u in range(NU):
                    self.done[chunk(3), u] = self.came(e, old, u, 2) + self.third(e, u, 3)

            @pl.when(both(live(2), not_late(2)))
            def _():
                for u in range(NU):
                    self.t2[e, u] = self.came(e, old, u, 1) + self.second(e, u, 3)
                    self.go(e, u, 2, self.third(e, u, 0))

            @pl.when(live(1))
            def _():
                own = self.own(chunk(1))
                for u in range(NU):
                    self.t1[e, u] = self.came(e, old, u, 0) + self.first(own, u, 3)
                    self.go(e, u, 1, self.second(e, u, 0))

            @pl.when(live(0))
            def _():
                self.ready(chunk(0))
                own = self.own(chunk(0))
                for u in range(NU):
                    self.go(e, u, 0, self.first(own, u, 0))
        else:
            @pl.when(ring2)
            def _():
                for u in range(NU):
                    self.go(e, u, 2, self.came(e, old, u, 2) + self.third(e, u, step))

            if drain and step == 1:
                @pl.when(middle)
                def _():
                    self.wait_straight(e, 2)
                    for u in range(NU):
                        self.done[chunk(2), u] = self.sum_straight(e, 2, u) + self.third(e, u, 3)

            @pl.when(ring1)
            def _():
                for u in range(NU):
                    self.go(e, u, 1, self.came(e, old, u, 1) + self.second(e, u, step))

            if drain:
                @pl.when(late)
                def _():
                    self.wait_straight(e, step - 1)
                    for u in range(NU):
                        if step == 1:
                            self.t2[e, u] = self.sum_straight(e, 0, u) + self.second(e, u, 3)
                        else:
                            self.done[chunk(1), u] = self.sum_straight(e, 1, u) + self.third(e, u, 3)

            @pl.when(live(0))
            def _():
                own = self.own(chunk(0))
                for u in range(NU):
                    self.go(e, u, 0, self.came(e, old, u, 0) + self.first(own, u, step))

        @pl.when(live(0))
        def _():
            self.send(e, par, 0)

        @pl.when(jnp.logical_not(live(0)) & (ring1 | ring2))
        def _():
            self.send(e, par, FROM[1])

        if drain and step < 2:
            @pl.when(late)
            def _():
                self.go_straight(e, step)

        if drain and step == 0:
            @pl.when(middle)
            def _():
                self.go_straight(e, 2)

    def step_of(self, s):
        return s * (STREAMS % PERIOD) % PERIOD if isinstance(s, int) else lax.rem(s * (STREAMS % PERIOD), PERIOD)

    def drain(self, start):
        def one(s, _):
            at = self.step_of(s)
            for step in range(PERIOD):
                @pl.when(at == step)
                def _():
                    self.slot(s, step, True)
            return 0

        lax.fori_loop(start, SLOTS - PERIOD + 5 * STREAMS + 1, one, 0)


def tiles_of_layer():
    down = [(3, g, j) for j in range(QUAD) for g in range(QUAD)]
    up = [(2, 0, j) for j in range(16)]
    out = [(1, 0, j) for j in range(QUAD)]
    qkv = [(0, 0, j) for j in range(12)]
    return down + up + out + qkv


TILES = tiles_of_layer()
PLACE_OF = {t: (i // 12, i % 12 // 6, i % 6) for i, t in enumerate(TILES)}


FWD_SEQS = 3
BWD_SEQS = 2
OWN_SLOTS = 6
LEAD = 2
QKV_W, OUT_W, UP_W, DOWN_W = range(4)
HALF = 2 * D
PIECES = [(QKV_W, ()), (OUT_W, ()), (UP_W, (slice(None), pl.ds(0, HALF))), (DOWN_W, (pl.ds(0, HALF),)),
          (UP_W, (slice(None), pl.ds(HALF, HALF))), (DOWN_W, (pl.ds(HALF, HALF),))]
ALL = range(len(PIECES))
QKV_P, OUT_P, UP_P, DOWN_P = (0,), (1,), (2, 4), (3, 5)


def step_kernel(x, seed, wq, wo, wu, wd,
                y, rq, ro, ru, rd, hs, qs, ps, os, ms, us, es, out,
                grads, recv, done, h, qkv, p, o, m, u, e, g, g1, do, vq, vo, vu, vd,
                wsem, asem, gsem, psem, qsem, hsem, ysem, dsend, drecv, fsem, credit, wfree, *ring):
    place = Place()
    core = place.core
    partner = place.partner()
    mine = (wq, wo, wu, wd)
    theirs = (rq, ro, ru, rd)
    held = (vq, vo, vu, vd)
    acts = ((h, hs), (qkv, qs), (p, ps), (o, os), (m, ms), (u, us), (e, es))
    H, QKV, PROB, O, M, U, E = range(7)
    rows = pl.ds(core * ROWS, ROWS)

    def to_partner(src, dst, send, arrive):
        return pltpu.make_async_remote_copy(src, dst, send, arrive, device_id=partner, device_id_type=MESH)

    def piece_of(ref, i):
        at = PIECES[i][1]
        return ref.at[at] if at else ref

    def push(i, j):
        k = PIECES[i][0]
        return to_partner(piece_of(mine[k].at[j], i), piece_of(theirs[k].at[j], i), psem.at[i, j], qsem.at[i, j])

    def hand(i, l):
        k = PIECES[i][0]
        return to_partner(piece_of(mine[k].at[l], i), piece_of(held[k], i), hsem.at[0, i], hsem.at[1, i])

    def local_w(i, l, src):
        k = PIECES[i][0]
        return pltpu.make_async_copy(piece_of(src[k].at[lax.rem(l, 2)], i), piece_of(held[k], i), wsem.at[i])

    def fetch_w(i, l, arrives):
        @pl.when(l // 2 == core)
        def _():
            local_w(i, l, mine).start()

        @pl.when(l // 2 != core)
        def _():
            @pl.when(arrives)
            def _():
                push(i, lax.rem(l, 2)).wait_recv()
            local_w(i, l, theirs).start()

    def wait_w(*pieces):
        for i in pieces:
            local_w(i, 0, mine).wait()

    def act(i, l, back):
        vmem, hbm = acts[i]
        return pltpu.make_async_copy(hbm.at[l], vmem, asem.at[i]) if back else pltpu.make_async_copy(vmem, hbm.at[l], asem.at[i])

    def own_slot(chunk):
        return lax.rem(chunk, OWN_SLOTS)

    def cross(chunk):
        q = lax.rem(chunk, QUAD)
        return to_partner(grads.at[OWN_SLOTS + q], recv.at[q], dsend.at[q], drecv.at[q])

    def ready(chunk):
        q = lax.rem(chunk, QUAD)
        cross(chunk).wait_recv()
        for unit in range(NU):
            grads[own_slot(chunk), unit] = grads[own_slot(chunk), unit] + recv[q, unit]

        @pl.when(chunk + QUAD < CHUNKS)
        def _():
            pl.semaphore_signal(credit.at[q], inc=1, device_id=partner, device_id_type=MESH)

    rings = Rings(place, ring, lambda chunk: grads.at[own_slot(chunk)], ready, done)

    x_in = pltpu.make_async_copy(x.at[rows], h, asem.at[H])
    x_in.start()
    seed_in = pltpu.make_async_copy(seed.at[rows], g, gsem)

    @pl.when(core == 0)
    def _():
        for i in ALL:
            local_w(i, 0, mine).start()
    greet([partner] + [place.neighbour(a, way) for a in NAT for way in (1, -1, 2)])

    @pl.when(core == 0)
    def _():
        for i in ALL:
            hand(i, 0).start()

    @pl.when(core == 1)
    def _():
        for j in range(2):
            for i in ALL:
                push(i, j).start()
    seed_in.start()
    x_in.wait()

    def layer(l, _):
        handed = (l < 2) & (core == 1)

        def weight(*pieces):
            @pl.when(jnp.logical_not(handed))
            def _():
                wait_w(*pieces)

            @pl.when(handed)
            def _():
                for i in pieces:
                    hand(i, 0).wait_recv()

        def used(group):
            @pl.when((l == 0) & (core == 1))
            def _():
                pl.semaphore_signal(wfree.at[group], inc=1, device_id=partner, device_id_type=MESH)

        def hand_on(at, group, *pieces):
            @pl.when((l == at) & (core == 0))
            def _():
                pl.semaphore_wait(wfree.at[group], 1)
                for i in pieces:
                    hand(i, 0).wait_send()
                    hand(i, 1).start()

        def again(i):
            @pl.when(l > 0)
            def _():
                act(i, l - 1, False).wait()

        def save(i):
            @pl.when(l < LAYERS - 1)
            def _():
                act(i, l, False).start()

        def next_w(when, to, *pieces):
            @pl.when(when)
            def _():
                for i in pieces:
                    fetch_w(i, to, True)

        more = l < LAYERS - 1
        again(H)

        @pl.when(l > 0)
        def _():
            h[...] = do[...]
        save(H)
        weight(0)
        again(QKV)
        hf = h[...].astype(F32)
        qkv[...] = dot((hf * inv_rms(hf)).astype(BF16), vq[...]).astype(BF16)
        used(0)
        hand_on(1, 2, 2, 3)
        save(QKV)
        again(PROB)
        again(O)

        def attend(i, _):
            attention_fwd(i, FWD_SEQS, qkv, p, o)
            return 0

        lax.fori_loop(0, NSEQ // FWD_SEQS, attend, 0)
        save(PROB)
        save(O)
        hand_on(1, 3, 4, 5)
        weight(1)
        again(M)
        m[...] = (h[...].astype(F32) + dot(o[...], vo[...])).astype(BF16)
        used(1)
        save(M)
        again(U)
        again(E)
        weight(2, 3)

        def mlp(j):
            cols = slice(j * HALF, (j + 1) * HALF)
            mf = m[...].astype(F32)
            c = (mf * inv_rms(mf)).astype(BF16)
            ub = dot(c, vu[:, cols]).astype(BF16)
            u[:, cols] = ub
            eb = gelu(ub.astype(F32)).astype(BF16)
            e[:, cols] = eb
            return dot(eb, vd[cols, :])

        half_way = m[...].astype(F32) + mlp(0)
        for unit in range(NU):
            for col in range(QUAD):
                grads[0, unit, :, :, col] = half_way[unit * SEQ:unit * SEQ + SEQ, col * LN:col * LN + LN].reshape(PLANE + TILE)
        used(2)
        mine_next = more & jnp.logical_or(l > 0, core == 0)
        next_w(mine_next, l + 1, 0, 1)
        weight(4, 5)
        rest = mlp(1)
        for unit in range(NU):
            part = pl.ds(unit * SEQ, SEQ)
            for col in range(QUAD):
                cols = slice(col * LN, col * LN + LN)
                do[part, cols] = (grads[0, unit, :, :, col].reshape((SEQ, LN)) + rest[unit * SEQ:unit * SEQ + SEQ, cols]).astype(BF16)
        used(3)
        hand_on(0, 0, 0)
        hand_on(0, 1, 1)
        next_w(mine_next, l + 1, 2, 3, 4, 5)

        @pl.when((l == 1) & (core == 0))
        def _():
            for j in (1, 0):
                for i in ALL:
                    push(i, j).start()
        save(U)
        save(E)
        return 0

    lax.fori_loop(0, LAYERS, layer, 0)
    y_here = pltpu.make_async_copy(do, y.at[rows], ysem.at[0])
    y_there = to_partner(do, y.at[rows], ysem.at[1], ysem.at[2])
    y_here.start()
    y_there.start()

    def free(chunk):
        @pl.when(chunk >= QUAD)
        def _():
            cross(chunk).wait_send()

    def put(base, tile, value):
        q, half, unit = PLACE_OF[tile]
        index = jnp.where(core == half, own_slot(base + q), OWN_SLOTS + q)
        grads[index, unit] = value.reshape(CUBE + TILE)

    def ship(chunk):
        @pl.when(chunk >= QUAD)
        def _():
            pl.semaphore_wait(credit.at[lax.rem(chunk, QUAD)], 1)
        cross(chunk).start()

    def down_grad(base):
        free(base)
        free(base + 1)
        for half in range(2):
            w = dot_first(e[...], g[:, half * 256:half * 256 + 256]).reshape((64, 4, 8, 256))
            for j in range(2):
                for rg in range(QUAD):
                    put(base, (DOWN_W, rg, 2 * half + j), w[:, rg, :, j * LN:j * LN + LN])
        ship(base)

    def gelu_part(lo, hi):
        de = dot_last(g[...], vd[lo:hi, :])
        u[:, lo:hi] = (gelu_slope(u[:, lo:hi].astype(F32)) * de).astype(BF16)

    def wide_grad(base, array, a, b, parts):
        for part in parts:
            w = dot_first(a, b[:, part * D:part * D + D]).reshape((64, 8, D))
            for j in range(QUAD):
                put(base, (array, 0, QUAD * part + j), w[:, :, j * LN:j * LN + LN])

    seed_in.wait()
    down_grad(0)
    act(E, LAYERS - 2, True).start()
    y_here.wait()
    y_there.wait_send()

    def iteration(it, _):
        l = LAYERS - 1 - it
        more = it < LAYERS - 1
        base = 4 * it

        def loaded(acts_of, pieces=()):
            @pl.when(it > 0)
            def _():
                for i in acts_of:
                    act(i, l, True).wait()
                wait_w(*pieces)

        def after(acts_of, pieces=()):
            @pl.when(more)
            def _():
                for i in pieces:
                    fetch_w(i, l - 1, l <= 2)
                for i in acts_of:
                    act(i, l - 1, True).start()

        def piece(n):
            if n == 0:
                loaded((U,), DOWN_P)
                gelu_part(0, 3 * 256)
            elif n == 1:
                gelu_part(3 * 256, 3 * D)
            elif n == 2:
                gelu_part(3 * D, QUAD * D)
                after((), DOWN_P)
                loaded((M,))
                mf = m[...].astype(F32)
                g1[...] = (mf * inv_rms(mf)).astype(BF16)
                wide_grad(base, UP_W, g1[...], u, (0,))
            elif n == 3:
                free(base + 2)
                wide_grad(base, UP_W, g1[...], u, (1, 2, 3))
                ship(base + 1)
            elif n == 4:
                loaded((), UP_P)
                dc = dot_last(u[...], vu[...])
                g1[...] = (g[...].astype(F32) + rms_bwd(m[...].astype(F32), dc)).astype(BF16)
                after((U, M), UP_P)
            elif n == 5:
                loaded((O,), OUT_P)
                do[...] = dot_last(g1[...], vo[...]).astype(BF16)
                wide_grad(base, OUT_W, o[...], g1, (0,))
                ship(base + 2)
                after((O,), OUT_P)
            elif n in (6, 7, 8):
                if n == 6:
                    loaded((PROB, QKV))
                attention_bwd(n - 6, BWD_SEQS, qkv, p, do)
                if n == 8:
                    after((PROB,))
            elif n == 9:
                loaded((H,))
                free(base + 3)
                hf = h[...].astype(F32)
                wide_grad(base, QKV_W, (hf * inv_rms(hf)).astype(BF16), qkv, (0, 1, 2))
                ship(base + 3)
            elif n == 10:
                loaded((), QKV_P)
                da = dot_last(qkv[...], vq[...])
                g[...] = (g1[...].astype(F32) + rms_bwd(h[...].astype(F32), da)).astype(BF16)
                after((H, QKV), QKV_P)
            else:
                @pl.when(more)
                def _():
                    act(E, l - 1, True).wait()
                    down_grad(base + QUAD)

                @pl.when(l > 1)
                def _():
                    act(E, l - 2, True).start()

        for n in range(12):
            s = 12 * it + n - LEAD
            step = rings.step_of(n + PERIOD - LEAD)
            if n < LEAD:
                @pl.when(it > 0)
                def _():
                    rings.slot(s, step)
            else:
                rings.slot(s, step)
            piece(n)
        return 0

    lax.fori_loop(0, LAYERS, iteration, 0)
    rings.drain(SLOTS - LEAD)

    for q in range(QUAD):
        cross(CHUNKS - 4 + q).wait_send()
    last = to_partner(done.at[pl.ds(8 * core, 8)], out.at[core], fsem.at[0], fsem.at[1])
    last.start()
    out[core] = done[pl.ds(8 * (1 - core), 8)]
    for j in range(2):
        for i in ALL:
            push(i, j).wait_send()

    @pl.when(core == 0)
    def _():
        for i in ALL:
            hand(i, 0).wait_send()
    y_there.wait_recv()
    last.wait_send()
    last.wait_recv()


def train_step(x, seed, weights):
    anywhere = pl.BlockSpec(memory_space=pl.ANY)
    vmem = pl.BlockSpec(memory_space=pltpu.VMEM)
    dma = pltpu.SemaphoreType.DMA
    act = lambda cols, dt=BF16: pltpu.VMEM((ROWS, cols), dt)
    saved = lambda cols, dt=BF16: jax.ShapeDtypeStruct((LAYERS - 1, ROWS, cols), dt)
    outs = pl.pallas_call(
        step_kernel,
        name="step",
        out_shape=[jax.ShapeDtypeStruct((2 * ROWS, D), BF16)] + [jax.ShapeDtypeStruct((2,) + s, BF16) for s in W_SHAPES]
        + [saved(D), saved(3 * D), saved(2 * D, F32), saved(D), saved(D), saved(QUAD * D), saved(QUAD * D)]
        + [jax.ShapeDtypeStruct((2, 8, NU) + TILE, F32)],
        in_specs=[anywhere] * 6,
        out_specs=[anywhere] * 12 + [vmem],
        scratch_shapes=[
            pltpu.VMEM((OWN_SLOTS + 4, NU) + CUBE + TILE, F32),
            pltpu.VMEM((4, NU) + CUBE + TILE, F32),
            pltpu.VMEM((CHUNKS, NU) + TILE, F32),
            act(D), act(3 * D), act(2 * D, F32), act(D), act(D), act(QUAD * D), act(QUAD * D), act(D), act(D), act(D),
        ] + [pltpu.VMEM(s, BF16) for s in W_SHAPES] + [
            dma((6,)), dma((7,)), dma, dma((6, 2)), dma((6, 2)), dma((2, 6)), dma((3,)), dma((QUAD,)), dma((QUAD,)), dma((2,)),
            pltpu.SemaphoreType.REGULAR((QUAD,)), pltpu.SemaphoreType.REGULAR((QUAD,)),
        ] + ring_scratch(),
        compiler_params=pltpu.CompilerParams(collective_id=1, has_side_effects=True, vmem_limit_bytes=67043328),
    )(x, seed, *weights)
    return outs[0], outs[-1]


def finish_kernel(y_in, sums, y, gq, go, gu, gd, buf, in_sem, out_sem):
    parts = buf.shape[0]
    move = lambda i, into: (pltpu.make_async_copy(y_in.at[i], buf.at[i], in_sem.at[i]) if into
                            else pltpu.make_async_copy(buf.at[i], y.at[i], out_sem.at[i]))
    for i in range(parts):
        move(i, True).start()
    outs = (gq, go, gu, gd)
    for layer in range(2):
        for tile in TILES:
            array, rg, col = tile
            q, half, unit = PLACE_OF[tile]
            outs[array][layer, rg * 8:rg * 8 + 8, col * LN:col * LN + LN] = sums[half, 4 * (1 - layer) + q, unit]
    for i in range(parts):
        move(i, True).wait()
        move(i, False).start()
    for i in range(parts):
        move(i, False).wait()


def finish(y, sums, parts=4):
    anywhere = pl.BlockSpec(memory_space=pl.ANY)
    vmem = pl.BlockSpec(memory_space=pltpu.VMEM)
    shape = (parts, 2 * ROWS // parts, D)
    return pl.pallas_call(
        finish_kernel,
        name="finish",
        out_shape=[jax.ShapeDtypeStruct(shape, BF16)]
        + [jax.ShapeDtypeStruct(s, F32) for s in ((2, 8, 3 * D), (2, 8, D), (2, 8, QUAD * D), (2, 32, D))],
        in_specs=[anywhere, vmem],
        out_specs=[anywhere] + [vmem] * 4,
        scratch_shapes=[pltpu.VMEM(shape, BF16), pltpu.SemaphoreType.DMA((parts,)), pltpu.SemaphoreType.DMA((parts,))],
    )(y.reshape(shape), sums)


def solution(mesh):
    def step(x_in, seed_grad, w_qkv, w_out, w_up, w_down):
        shape = x_in.shape
        weights = (w_qkv, w_out, w_up, w_down)
        y, sums = train_step(x_in.reshape(2 * ROWS, D), seed_grad.reshape(2 * ROWS, D), weights)
        y, *grads = finish(y, sums)
        return y.reshape(shape), *grads

    act, weight, grad = P(None, "dp"), P("pp"), P("pp", "dp")
    return jax.shard_map(
        step,
        mesh=mesh,
        in_specs=(act, act, weight, weight, weight, weight),
        out_specs=(act, grad, grad, grad, grad),
        check_vma=False,
    )
```

time: 192 us -> 174 us (0.906)
  Pallas kernels: 191 us -> 173 us
    pallas_call x1, Pallas kernels: 187 us -> 169 us  [train_step(): pl.pallas_call(step_kernel, name='step', out_shape=[jax.ShapeDtypeStruct(...]
where the time goes in v3:
time: 174 us
  Pallas kernels  173 us (99%)
    pallas_call x1, Pallas kernels, train_step(): pl.pallas_call(step_kernel, name='step', out_shape=[jax.ShapeDtypeStruct(...  169 us
    pallas_call x1, Pallas kernels, finish(): pl.pallas_call(finish_kernel, name='finish', out_shape=[jax.ShapeDtypeStr...  3.94 us

profile of v3, /device:TPU:1, one launch (start us, length us, event | category | flops | bytes accessed | tf_op | source)
XLA Modules:
  0.0 174.0 jit_solution(2783840901414549897)
XLA Ops:
  0.6 169.2 %step.1 = (bf16[1536,512]{1,0:T(8,128)(2,1)}, bf16[2,512,1536]{2,1,0:T(8,128)(2,1)}, bf16[2,512,512]{2,1,0:T(8,128)(2,1)}, bf16[2,512,2048]{2,1,0:T(8,128)(2,1)}...) custom-call(bf16[1536,512]{1,0:T(8,128)(2,1)} %bitcast.7, ...), custom_call_target="tpu_custom_call" | custom-call | tf_op jit(solution)/shard_map/step/pallas_call | solution.py:785
  169.9 3.9 %finish.1 = (bf16[4,384,512]{2,1,0:T(8,128)(2,1)}, f32[2,8,1536]{2,1,0:T(8,128)}, f32[2,8,512]{2,1,0:T(8,128)}, f32[2,8,2048]{2,1,0:T(8,128)}, f32[2,32,512]{2,1,0:T(8,128)}) custom-call(bf16[4,384,512]{2,1,0:T(8,128)(2,1)} %bitcast.6, f32[2,8,6,8,128]{4,3,2,1,0:T(8,128)} %get-tuple-element.13.sums), custom_call_target="tpu_custom_call" | custom-call | tf_op jit(solution)/shard_map/finish/pallas_call | solution.py:830

commit v4 on v3

--- a/solution.py
+++ b/solution.py
@@ -399,10 +399,11 @@
 PLACE_OF = {t: (i // 12, i % 12 // 6, i % 6) for i, t in enumerate(TILES)}
 
 
-FWD_SEQS = 3
-BWD_SEQS = 2
-OWN_SLOTS = 6
-LEAD = 2
+FWD_SEQS = 6
+BWD_SEQS = 3
+OWN_SLOTS = 7
+SENT_SLOTS = 3
+LEAD = 3
 QKV_W, OUT_W, UP_W, DOWN_W = range(4)
 HALF = 2 * D
 PIECES = [(QKV_W, ()), (OUT_W, ()), (UP_W, (slice(None), pl.ds(0, HALF))), (DOWN_W, (pl.ds(0, HALF),)),
@@ -467,17 +468,20 @@
     def own_slot(chunk):
         return lax.rem(chunk, OWN_SLOTS)
 
+    def sent_slot(chunk):
+        return lax.rem(chunk, SENT_SLOTS)
+
     def cross(chunk):
-        q = lax.rem(chunk, QUAD)
+        q = sent_slot(chunk)
         return to_partner(grads.at[OWN_SLOTS + q], recv.at[q], dsend.at[q], drecv.at[q])
 
     def ready(chunk):
-        q = lax.rem(chunk, QUAD)
+        q = sent_slot(chunk)
         cross(chunk).wait_recv()
         for unit in range(NU):
             grads[own_slot(chunk), unit] = grads[own_slot(chunk), unit] + recv[q, unit]
 
-        @pl.when(chunk + QUAD < CHUNKS)
+        @pl.when(chunk + SENT_SLOTS < CHUNKS)
         def _():
             pl.semaphore_signal(credit.at[q], inc=1, device_id=partner, device_id_type=MESH)
 
@@ -560,22 +564,22 @@
         hf = h[...].astype(F32)
         qkv[...] = dot((hf * inv_rms(hf)).astype(BF16), vq[...]).astype(BF16)
         used(0)
-        hand_on(1, 2, 2, 3)
         save(QKV)
         again(PROB)
         again(O)
 
-        def attend(i, _):
+        for i in range(NSEQ // FWD_SEQS):
             attention_fwd(i, FWD_SEQS, qkv, p, o)
-            return 0
-
-        lax.fori_loop(0, NSEQ // FWD_SEQS, attend, 0)
+        hand_on(0, 0, 0)
+        hand_on(1, 3, 4, 5)
         save(PROB)
         save(O)
-        hand_on(1, 3, 4, 5)
         weight(1)
         again(M)
-        m[...] = (h[...].astype(F32) + dot(o[...], vo[...])).astype(BF16)
+        mb = (h[...].astype(F32) + dot(o[...], vo[...])).astype(BF16)
+        m[...] = mb
+        mf = mb.astype(F32)
+        g1[...] = (mf * inv_rms(mf)).astype(BF16)
         used(1)
         save(M)
         again(U)
@@ -584,9 +588,7 @@
 
         def mlp(j):
             cols = slice(j * HALF, (j + 1) * HALF)
-            mf = m[...].astype(F32)
-            c = (mf * inv_rms(mf)).astype(BF16)
-            ub = dot(c, vu[:, cols]).astype(BF16)
+            ub = dot(g1[...], vu[:, cols]).astype(BF16)
             u[:, cols] = ub
             eb = gelu(ub.astype(F32)).astype(BF16)
             e[:, cols] = eb
@@ -597,6 +599,7 @@
             for col in range(QUAD):
                 grads[0, unit, :, :, col] = half_way[unit * SEQ:unit * SEQ + SEQ, col * LN:col * LN + LN].reshape(PLANE + TILE)
         used(2)
+        hand_on(0, 1, 1)
         mine_next = more & jnp.logical_or(l > 0, core == 0)
         next_w(mine_next, l + 1, 0, 1)
         weight(4, 5)
@@ -607,8 +610,7 @@
                 cols = slice(col * LN, col * LN + LN)
                 do[part, cols] = (grads[0, unit, :, :, col].reshape((SEQ, LN)) + rest[unit * SEQ:unit * SEQ + SEQ, cols]).astype(BF16)
         used(3)
-        hand_on(0, 0, 0)
-        hand_on(0, 1, 1)
+        hand_on(0, 2, 2, 3)
         next_w(mine_next, l + 1, 2, 3, 4, 5)
 
         @pl.when((l == 1) & (core == 0))
@@ -627,30 +629,32 @@
     y_there.start()
 
     def free(chunk):
-        @pl.when(chunk >= QUAD)
+        @pl.when(chunk >= SENT_SLOTS)
         def _():
             cross(chunk).wait_send()
 
     def put(base, tile, value):
         q, half, unit = PLACE_OF[tile]
-        index = jnp.where(core == half, own_slot(base + q), OWN_SLOTS + q)
+        index = jnp.where(core == half, own_slot(base + q), OWN_SLOTS + sent_slot(base + q))
         grads[index, unit] = value.reshape(CUBE + TILE)
 
     def ship(chunk):
-        @pl.when(chunk >= QUAD)
-        def _():
-            pl.semaphore_wait(credit.at[lax.rem(chunk, QUAD)], 1)
+        @pl.when(chunk >= SENT_SLOTS)
+        def _():
+            pl.semaphore_wait(credit.at[sent_slot(chunk)], 1)
         cross(chunk).start()
 
-    def down_grad(base):
-        free(base)
-        free(base + 1)
-        for half in range(2):
-            w = dot_first(e[...], g[:, half * 256:half * 256 + 256]).reshape((64, 4, 8, 256))
+    def down_grad(base, halves):
+        for half in halves:
+            if half == 0:
+                free(base)
+                free(base + 1)
+            w = dot_first(e[...], g[:, half * 256:half * 256 + 256]).reshape((64, QUAD, 8, 256))
             for j in range(2):
                 for rg in range(QUAD):
                     put(base, (DOWN_W, rg, 2 * half + j), w[:, rg, :, j * LN:j * LN + LN])
-        ship(base)
+            if half == 1:
+                ship(base)
 
     def gelu_part(lo, hi):
         de = dot_last(g[...], vd[lo:hi, :])
@@ -663,7 +667,7 @@
                 put(base, (array, 0, QUAD * part + j), w[:, :, j * LN:j * LN + LN])
 
     seed_in.wait()
-    down_grad(0)
+    down_grad(0, range(2))
     act(E, LAYERS - 2, True).start()
     y_here.wait()
     y_there.wait_send()
@@ -716,19 +720,19 @@
                 wide_grad(base, OUT_W, o[...], g1, (0,))
                 ship(base + 2)
                 after((O,), OUT_P)
-            elif n in (6, 7, 8):
+            elif n in (6, 7):
                 if n == 6:
                     loaded((PROB, QKV))
                 attention_bwd(n - 6, BWD_SEQS, qkv, p, do)
-                if n == 8:
+                if n == 7:
                     after((PROB,))
-            elif n == 9:
+            elif n == 8:
                 loaded((H,))
                 free(base + 3)
                 hf = h[...].astype(F32)
-                wide_grad(base, QKV_W, (hf * inv_rms(hf)).astype(BF16), qkv, (0, 1, 2))
+                wide_grad(base, QKV_W, (hf * inv_rms(hf)).astype(BF16), qkv, range(3))
                 ship(base + 3)
-            elif n == 10:
+            elif n == 9:
                 loaded((), QKV_P)
                 da = dot_last(qkv[...], vq[...])
                 g[...] = (g1[...].astype(F32) + rms_bwd(h[...].astype(F32), da)).astype(BF16)
@@ -736,16 +740,18 @@
             else:
                 @pl.when(more)
                 def _():
-                    act(E, l - 1, True).wait()
-                    down_grad(base + QUAD)
-
-                @pl.when(l > 1)
-                def _():
-                    act(E, l - 2, True).start()
+                    if n == 10:
+                        act(E, l - 1, True).wait()
+                    down_grad(base + QUAD, (n - 10,))
+
+                if n == 11:
+                    @pl.when(l > 1)
+                    def _():
+                        act(E, l - 2, True).start()
 
         for n in range(12):
             s = 12 * it + n - LEAD
-            step = rings.step_of(n + PERIOD - LEAD)
+            step = rings.step_of(n + 2 * PERIOD - LEAD)
             if n < LEAD:
                 @pl.when(it > 0)
                 def _():
@@ -758,11 +764,12 @@
     lax.fori_loop(0, LAYERS, iteration, 0)
     rings.drain(SLOTS - LEAD)
 
-    for q in range(QUAD):
-        cross(CHUNKS - 4 + q).wait_send()
+    for q in range(SENT_SLOTS):
+        cross(q).wait_send()
     last = to_partner(done.at[pl.ds(8 * core, 8)], out.at[core], fsem.at[0], fsem.at[1])
     last.start()
-    out[core] = done[pl.ds(8 * (1 - core), 8)]
+    kept = pltpu.make_async_copy(done.at[pl.ds(8 * (1 - core), 8)], out.at[core], gsem)
+    kept.start()
     for j in range(2):
         for i in ALL:
             push(i, j).wait_send()
@@ -772,13 +779,13 @@
         for i in ALL:
             hand(i, 0).wait_send()
     y_there.wait_recv()
+    kept.wait()
     last.wait_send()
     last.wait_recv()
 
 
 def train_step(x, seed, weights):
     anywhere = pl.BlockSpec(memory_space=pl.ANY)
-    vmem = pl.BlockSpec(memory_space=pltpu.VMEM)
     dma = pltpu.SemaphoreType.DMA
     act = lambda cols, dt=BF16: pltpu.VMEM((ROWS, cols), dt)
     saved = lambda cols, dt=BF16: jax.ShapeDtypeStruct((LAYERS - 1, ROWS, cols), dt)
@@ -789,10 +796,10 @@
         + [saved(D), saved(3 * D), saved(2 * D, F32), saved(D), saved(D), saved(QUAD * D), saved(QUAD * D)]
         + [jax.ShapeDtypeStruct((2, 8, NU) + TILE, F32)],
         in_specs=[anywhere] * 6,
-        out_specs=[anywhere] * 12 + [vmem],
+        out_specs=[anywhere] * 13,
         scratch_shapes=[
-            pltpu.VMEM((OWN_SLOTS + 4, NU) + CUBE + TILE, F32),
-            pltpu.VMEM((4, NU) + CUBE + TILE, F32),
+            pltpu.VMEM((OWN_SLOTS + SENT_SLOTS, NU) + CUBE + TILE, F32),
+            pltpu.VMEM((SENT_SLOTS, NU) + CUBE + TILE, F32),
             pltpu.VMEM((CHUNKS, NU) + TILE, F32),
             act(D), act(3 * D), act(2 * D, F32), act(D), act(D), act(QUAD * D), act(QUAD * D), act(D), act(D), act(D),
         ] + [pltpu.VMEM(s, BF16) for s in W_SHAPES] + [
@@ -804,37 +811,41 @@
     return outs[0], outs[-1]
 
 
-def finish_kernel(y_in, sums, y, gq, go, gu, gd, buf, in_sem, out_sem):
+def finish_kernel(y_in, sums_in, y, gq, go, gu, gd, buf, sums, in_sem, out_sem, sum_sem):
     parts = buf.shape[0]
-    move = lambda i, into: (pltpu.make_async_copy(y_in.at[i], buf.at[i], in_sem.at[i]) if into
-                            else pltpu.make_async_copy(buf.at[i], y.at[i], out_sem.at[i]))
-    for i in range(parts):
-        move(i, True).start()
+    here = pltpu.make_async_copy(sums_in, sums, sum_sem)
+    here.start()
+    into = [pltpu.make_async_copy(y_in.at[i], buf.at[i], in_sem.at[i]) for i in range(parts)]
+    out = [pltpu.make_async_copy(buf.at[i], y.at[i], out_sem.at[i]) for i in range(parts)]
+    for c in into:
+        c.start()
+    here.wait()
     outs = (gq, go, gu, gd)
     for layer in range(2):
         for tile in TILES:
             array, rg, col = tile
             q, half, unit = PLACE_OF[tile]
-            outs[array][layer, rg * 8:rg * 8 + 8, col * LN:col * LN + LN] = sums[half, 4 * (1 - layer) + q, unit]
-    for i in range(parts):
-        move(i, True).wait()
-        move(i, False).start()
-    for i in range(parts):
-        move(i, False).wait()
-
-
-def finish(y, sums, parts=4):
+            outs[array][layer, rg * 8:rg * 8 + 8, col * LN:col * LN + LN] = sums[half, QUAD * (1 - layer) + q, unit]
+    for c, d in zip(into, out):
+        c.wait()
+        d.start()
+    for d in out:
+        d.wait()
+
+
+def finish(y, sums, parts=6):
     anywhere = pl.BlockSpec(memory_space=pl.ANY)
     vmem = pl.BlockSpec(memory_space=pltpu.VMEM)
+    dma = pltpu.SemaphoreType.DMA
     shape = (parts, 2 * ROWS // parts, D)
     return pl.pallas_call(
         finish_kernel,
         name="finish",
         out_shape=[jax.ShapeDtypeStruct(shape, BF16)]
         + [jax.ShapeDtypeStruct(s, F32) for s in ((2, 8, 3 * D), (2, 8, D), (2, 8, QUAD * D), (2, 32, D))],
-        in_specs=[anywhere, vmem],
-        out_specs=[anywhere] + [vmem] * 4,
-        scratch_shapes=[pltpu.VMEM(shape, BF16), pltpu.SemaphoreType.DMA((parts,)), pltpu.SemaphoreType.DMA((parts,))],
+        in_specs=[anywhere] * 2,
+        out_specs=[anywhere] + [vmem] * QUAD,
+        scratch_shapes=[pltpu.VMEM(shape, BF16), pltpu.VMEM(sums.shape, F32), dma((parts,)), dma((parts,)), dma],
     )(y.reshape(shape), sums)
 
 

time: 174 us -> 166 us (0.954)
  Pallas kernels: 173 us -> 165 us
    pallas_call x1, Pallas kernels: 169 us -> 162 us  [train_step(): pl.pallas_call(step_kernel, name='step', out_shape=[jax.ShapeDtypeStruct(...]
where the time goes in v4:
time: 166 us
  Pallas kernels  165 us (99%)
    pallas_call x1, Pallas kernels, train_step(): pl.pallas_call(step_kernel, name='step', out_shape=[jax.ShapeDtypeStruct(...  162 us
    pallas_call x1, Pallas kernels, finish(): pl.pallas_call(finish_kernel, name='finish', out_shape=[jax.ShapeDtypeStr...  3.41 us

profile of v4, /device:TPU:1, one launch (start us, length us, event | category | flops | bytes accessed | tf_op | source)
XLA Modules:
  0.0 166.2 jit_solution(10945590794149718249)
XLA Ops:
  0.6 162.0 %step.1 = (bf16[1536,512]{1,0:T(8,128)(2,1)}, bf16[2,512,1536]{2,1,0:T(8,128)(2,1)}, bf16[2,512,512]{2,1,0:T(8,128)(2,1)}, bf16[2,512,2048]{2,1,0:T(8,128)(2,1)}...) custom-call(bf16[1536,512]{1,0:T(8,128)(2,1)} %bitcast.7, ...), custom_call_target="tpu_custom_call" | custom-call | tf_op jit(solution)/shard_map/step/pallas_call | solution.py:792
  162.7 3.4 %finish.1 = (bf16[6,256,512]{2,1,0:T(8,128)(2,1)}, f32[2,8,1536]{2,1,0:T(8,128)}, f32[2,8,512]{2,1,0:T(8,128)}, f32[2,8,2048]{2,1,0:T(8,128)}, f32[2,32,512]{2,1,0:T(8,128)}) custom-call(bf16[6,256,512]{2,1,0:T(8,128)(2,1)} %bitcast.6, f32[2,8,6,8,128]{4,3,2,1,0:T(8,128)} %get-tuple-element.13.sums_in), custom_call_target="tpu_custom_call" | custom-call | tf_op jit(solution)/shard_map/finish/pallas_call | solution.py:841

commit v5 on v4

--- a/solution.py
+++ b/solution.py
@@ -811,7 +811,10 @@
     return outs[0], outs[-1]
 
 
-def finish_kernel(y_in, sums_in, y, gq, go, gu, gd, buf, sums, in_sem, out_sem, sum_sem):
+ROW_SHAPES = ((2, 8, 3 * D), (2, 8, D), (2, 8, QUAD * D), (2, 32, D))
+
+
+def finish_kernel(y_in, sums_in, y, gq, go, gu, gd, buf, sums, bq, bo, bu, bd, in_sem, out_sem, sum_sem, grad_sem):
     parts = buf.shape[0]
     here = pltpu.make_async_copy(sums_in, sums, sum_sem)
     here.start()
@@ -820,32 +823,34 @@
     for c in into:
         c.start()
     here.wait()
-    outs = (gq, go, gu, gd)
+    rows = (bq, bo, bu, bd)
     for layer in range(2):
         for tile in TILES:
             array, rg, col = tile
             q, half, unit = PLACE_OF[tile]
-            outs[array][layer, rg * 8:rg * 8 + 8, col * LN:col * LN + LN] = sums[half, QUAD * (1 - layer) + q, unit]
+            rows[array][layer, rg * 8:rg * 8 + 8, col * LN:col * LN + LN] = sums[half, QUAD * (1 - layer) + q, unit]
+    out += [pltpu.make_async_copy(r, o, grad_sem.at[i]) for i, (r, o) in enumerate(zip(rows, (gq, go, gu, gd)))]
     for c, d in zip(into, out):
         c.wait()
         d.start()
+    for d in out[parts:]:
+        d.start()
     for d in out:
         d.wait()
 
 
 def finish(y, sums, parts=6):
     anywhere = pl.BlockSpec(memory_space=pl.ANY)
-    vmem = pl.BlockSpec(memory_space=pltpu.VMEM)
     dma = pltpu.SemaphoreType.DMA
     shape = (parts, 2 * ROWS // parts, D)
     return pl.pallas_call(
         finish_kernel,
         name="finish",
-        out_shape=[jax.ShapeDtypeStruct(shape, BF16)]
-        + [jax.ShapeDtypeStruct(s, F32) for s in ((2, 8, 3 * D), (2, 8, D), (2, 8, QUAD * D), (2, 32, D))],
+        out_shape=[jax.ShapeDtypeStruct(shape, BF16)] + [jax.ShapeDtypeStruct(s, F32) for s in ROW_SHAPES],
         in_specs=[anywhere] * 2,
-        out_specs=[anywhere] + [vmem] * QUAD,
-        scratch_shapes=[pltpu.VMEM(shape, BF16), pltpu.VMEM(sums.shape, F32), dma((parts,)), dma((parts,)), dma],
+        out_specs=[anywhere] * 5,
+        scratch_shapes=[pltpu.VMEM(shape, BF16), pltpu.VMEM(sums.shape, F32)] + [pltpu.VMEM(s, F32) for s in ROW_SHAPES]
+        + [dma((parts,)), dma((parts,)), dma, dma((QUAD,))],
     )(y.reshape(shape), sums)
 
 

time: 166 us -> 166 us (level)
  no operation moved by 1% of the time
where the time goes in v5:
time: 166 us
  Pallas kernels  165 us (99%)
    pallas_call x1, Pallas kernels, train_step(): pl.pallas_call(step_kernel, name='step', out_shape=[jax.ShapeDtypeStruct(...  162 us

profile of v5, /device:TPU:1, one launch (start us, length us, event | category | flops | bytes accessed | tf_op | source)
XLA Modules:
  0.0 165.7 jit_solution(9478033451741659193)
XLA Ops:
  0.6 162.0 %step.1 = (bf16[1536,512]{1,0:T(8,128)(2,1)}, bf16[2,512,1536]{2,1,0:T(8,128)(2,1)}, bf16[2,512,512]{2,1,0:T(8,128)(2,1)}, bf16[2,512,2048]{2,1,0:T(8,128)(2,1)}...) custom-call(bf16[1536,512]{1,0:T(8,128)(2,1)} %bitcast.7, ...), custom_call_target="tpu_custom_call" | custom-call | tf_op jit(solution)/shard_map/step/pallas_call | solution.py:792
  162.7 2.8 %finish.1 = (bf16[6,256,512]{2,1,0:T(8,128)(2,1)}, f32[2,8,1536]{2,1,0:T(8,128)}, f32[2,8,512]{2,1,0:T(8,128)}, f32[2,8,2048]{2,1,0:T(8,128)}, f32[2,32,512]{2,1,0:T(8,128)}) custom-call(bf16[6,256,512]{2,1,0:T(8,128)(2,1)} %bitcast.6, f32[2,8,6,8,128]{4,3,2,1,0:T(8,128)} %get-tuple-element.13.sums_in), custom_call_target="tpu_custom_call" | custom-call | tf_op jit(solution)/shard_map/finish/pallas_call | solution.py:846

commit v6 on v5

--- a/solution.py
+++ b/solution.py
@@ -251,7 +251,7 @@
         return self.d2.at[e] if kind == 0 else self.d3.at[kind - 1, e]
 
     def go_straight(self, e, kind):
-        for j in (1, 3, 2):
+        for j in (2, 1, 3):
             for u in range(NU):
                 self.straight(e, kind, u, j).start()
 
@@ -399,7 +399,6 @@
 PLACE_OF = {t: (i // 12, i % 12 // 6, i % 6) for i, t in enumerate(TILES)}
 
 
-FWD_SEQS = 6
 BWD_SEQS = 3
 OWN_SLOTS = 7
 SENT_SLOTS = 3
@@ -560,20 +559,16 @@
             h[...] = do[...]
         save(H)
         weight(0)
-        again(QKV)
+        for i in (QKV, PROB, O):
+            again(i)
         hf = h[...].astype(F32)
         qkv[...] = dot((hf * inv_rms(hf)).astype(BF16), vq[...]).astype(BF16)
+        attention_fwd(0, NSEQ, qkv, p, o)
         used(0)
-        save(QKV)
-        again(PROB)
-        again(O)
-
-        for i in range(NSEQ // FWD_SEQS):
-            attention_fwd(i, FWD_SEQS, qkv, p, o)
         hand_on(0, 0, 0)
         hand_on(1, 3, 4, 5)
-        save(PROB)
-        save(O)
+        for i in (QKV, PROB, O):
+            save(i)
         weight(1)
         again(M)
         mb = (h[...].astype(F32) + dot(o[...], vo[...])).astype(BF16)

time: 166 us -> 166 us (level)
  no operation moved by 1% of the time
where the time goes in v6:
time: 166 us
  Pallas kernels  165 us (99%)
    pallas_call x1, Pallas kernels, train_step(): pl.pallas_call(step_kernel, name='step', out_shape=[jax.ShapeDtypeStruct(...  162 us

profile of v6, /device:TPU:1, one launch (start us, length us, event | category | flops | bytes accessed | tf_op | source)
XLA Modules:
  0.0 166.1 jit_solution(16257119414677363934)
XLA Ops:
  0.6 162.5 %step.1 = (bf16[1536,512]{1,0:T(8,128)(2,1)}, bf16[2,512,1536]{2,1,0:T(8,128)(2,1)}, bf16[2,512,512]{2,1,0:T(8,128)(2,1)}, bf16[2,512,2048]{2,1,0:T(8,128)(2,1)}...) custom-call(bf16[1536,512]{1,0:T(8,128)(2,1)} %bitcast.7, ...), custom_call_target="tpu_custom_call" | custom-call | tf_op jit(solution)/shard_map/step/pallas_call | solution.py:787
  163.1 2.8 %finish.1 = (bf16[6,256,512]{2,1,0:T(8,128)(2,1)}, f32[2,8,1536]{2,1,0:T(8,128)}, f32[2,8,512]{2,1,0:T(8,128)}, f32[2,8,2048]{2,1,0:T(8,128)}, f32[2,32,512]{2,1,0:T(8,128)}) custom-call(bf16[6,256,512]{2,1,0:T(8,128)(2,1)} %bitcast.6, f32[2,8,6,8,128]{4,3,2,1,0:T(8,128)} %get-tuple-element.13.sums_in), custom_call_target="tpu_custom_call" | custom-call | tf_op jit(solution)/shard_map/finish/pallas_call | solution.py:841
